TPU v7x, 32 devices: a whole 2x2x4 slice. The times are simulated.
32 devices in a mesh: seq: 4 (over z), tp: 4 (over y, x), dp: 2 (over core).
Axes of the slice: x: 2, y: 2, z: 4, core: 2. Of those that a mesh axis runs over, the one named last changes fastest.
Arguments:
- x_ckpt: bfloat16 [1024, 5120], P(('dp', 'seq', 'tp')), parts along dimension 0, may hold values from -5 to 5
- bc_ckpt: bfloat16 [2, 1024, 128], P(None, ('dp', 'seq', 'tp')), parts along dimension 1, may hold values from -1 to 1
- step_sizes: float32 [80, 1024], P('tp', ('dp', 'seq')), parts along dimension 1, may hold values from 0.03 to 0.3
- decay_rate: float32 [80], P('tp'), may hold values from 0 to 1, as said below
- skip_gain: float32 [80], P('tp'), may hold values from 0.25 to 1.75
- grad_out: bfloat16 [1024, 5120], P(('dp', 'seq'), 'tp'), parts along dimension 0, may hold values from -3 to 3
Outputs:
- grad_x: bfloat16 [1024, 5120], P(('dp', 'seq'), 'tp'), parts along dimension 0
- grad_bc: float32 [2, 1024, 128], P(None, ('dp', 'seq', 'tp')), parts along dimension 1
- grad_step: float32 [80, 1024], P('tp', ('dp', 'seq')), parts along dimension 1
There are 2 independent parts, one for each index of `dp`. A program takes and returns all parts, laid end to end along the dimension named above; an argument that names none is the same for every part. Nothing has to cross between parts.
Inputs may be any that keep to these rules, and one draw needn't show every extreme that they name: `decay_rate`: positive decay rates of the 80 heads.
All inputs are finite; a program needn't handle non-finite values.
Results may differ from a plain program's by a relative error of at most 0.001.
Values may be sent and summed in bfloat16 or wider, within the bound.
A program may use at most 128 MiB of HBM per device.

v0:
```python
from functools import partial

import jax
import jax.numpy as jnp
from jax import lax
from jax.experimental import pallas as pl
from jax.experimental.pallas import tpu as pltpu
from jax.sharding import PartitionSpec as P

MESH = pl.DeviceIdType.MESH
F32 = jnp.float32
BF16 = jnp.bfloat16
HEAD_PAD = 32
SKEW = 3

NN = (((1,), (0,)), ((), ()))
NT = (((1,), (1,)), ((), ()))


def dot(a, b, dims=NN):
    return lax.dot_general(a, b, dims, preferred_element_type=F32)


def exact(a, b):
    return lax.dot_general(
        a, b, NN, precision=lax.Precision.HIGHEST, preferred_element_type=F32
    )


def split(v):
    high = v.astype(BF16)
    return high, (v - high.astype(F32)).astype(BF16)


def joined(a, b, dims=NN):
    return dot(jnp.concatenate(a, axis=1), jnp.concatenate(b, axis=dims[0][1][0]), dims)


def dot2(a, b, dims=NN):
    return joined((a, a), b, dims)


def dot2l(a, b, dims=NN):
    return joined(a, (b, b), dims)


def dot3(a, b, dims=NN):
    return joined((a[0], a[0], a[1]), (b[0], b[1], b[0]), dims)


def kernel(
    peers, blocks, head_width,
    x_ref, bc_ref, step_ref, rate_ref, gain_ref, dy_ref,
    gx_ref, gbc_ref, gstep_ref,
    xr, bcr, part, rs,
    state_in, state_out, pull_in, pull_out, fresh, pulled,
    xs_h, xs_l, ys_h, ys_l, xc, dyc, ec, ed, gain_row,
    stp, rates, gains, cums, mt_acc, bc_acc, dcum_acc, dir_acc, sm, bcm,
    send_x, recv_x, send_b, recv_b, own_sem,
    send_f, recv_f, send_g, recv_g, send_r, recv_r,
):
    me = lax.axis_index("tp")
    block = lax.axis_index("seq")
    head_count, tokens = step_ref.shape
    width = dy_ref.shape[1]
    rows = x_ref.shape[0]
    chunks, _, lanes = xc.shape
    chunk_heads = lanes // head_width

    has_prev = block > 0
    has_next = block < blocks - 1

    barrier = pltpu.get_barrier_semaphore()
    for d in range(1, peers):
        pl.semaphore_signal(
            barrier, inc=1, device_id={"tp": lax.rem(me + d, peers)}, device_id_type=MESH
        )

    @pl.when(has_prev)
    def _():
        pl.semaphore_signal(barrier, inc=1, device_id={"seq": block - 1}, device_id_type=MESH)

    @pl.when(has_next)
    def _():
        pl.semaphore_signal(barrier, inc=1, device_id={"seq": block + 1}, device_id_type=MESH)

    neighbours = jnp.where(has_prev, 1, 0) + jnp.where(has_next, 1, 0)
    pl.semaphore_wait(barrier, peers - 1 + neighbours)

    def bc_copy(peer, slot):
        return pltpu.make_async_remote_copy(
            src_ref=bc_ref, dst_ref=bcr.at[slot],
            send_sem=send_b.at[peer], recv_sem=recv_b.at[slot],
            device_id={"tp": peer}, device_id_type=MESH,
        )

    def x_copy(peer, slot):
        return pltpu.make_async_remote_copy(
            src_ref=x_ref.at[:, pl.ds(pl.multiple_of(peer * width, 128), width)],
            dst_ref=xr.at[slot],
            send_sem=send_x.at[peer], recv_sem=recv_x.at[slot],
            device_id={"tp": peer}, device_id_type=MESH,
        )

    for d in range(1, peers):
        bc_copy(lax.rem(me + d, peers), me).start()
    for d in range(1, peers):
        x_copy(lax.rem(me + d, peers), me).start()
    own_x = pltpu.make_async_copy(
        x_ref.at[:, pl.ds(pl.multiple_of(me * width, 128), width)], xr.at[me], own_sem.at[0]
    )
    own_bc = pltpu.make_async_copy(bc_ref, bcr.at[me], own_sem.at[1])
    own_x.start()
    own_bc.start()

    stp[...] = jnp.zeros_like(stp)
    stp[0:head_count] = step_ref[...]
    rates[...] = jnp.zeros_like(rates)
    gains[...] = jnp.zeros_like(gains)
    for h in range(head_count):
        rates[h : h + 1] = jnp.full((1, tokens), rate_ref[h], F32)
        gains[h : h + 1] = jnp.full((1, tokens), gain_ref[h], F32)
    row = lax.broadcasted_iota(jnp.int32, (tokens, tokens), 0)
    col = lax.broadcasted_iota(jnp.int32, (tokens, tokens), 1)
    upto = row <= col
    cum = exact(-rates[...] * stp[...], jnp.where(upto, 1.0, 0.0).astype(F32))
    cums[...] = cum
    stacked = jnp.concatenate(
        [jnp.exp(cum), jnp.exp(-cum) * stp[...], gains[...], jnp.zeros_like(cum)], axis=0
    )
    table = split(stacked.T)
    pick_row = lax.broadcasted_iota(jnp.int32, (4 * HEAD_PAD, lanes), 0)
    pick_head = lax.broadcasted_iota(jnp.int32, (4 * HEAD_PAD, lanes), 1) // head_width
    for c in range(chunks):
        def spread(q):
            hit = pick_row == (q * HEAD_PAD + c * chunk_heads) + pick_head
            return jnp.where(hit, 1.0, 0.0).astype(BF16)

        grown = dot2l(table, spread(0))
        ec[c] = grown
        ed[c] = dot2l(table, spread(1))
        gain_row[c] = dot2l((table[0][0:16], table[1][0:16]), spread(2))[0:8]
        dy = dy_ref[:, c * lanes : (c + 1) * lanes]
        dyc[c] = dy
        high, low = split(grown * dy.astype(F32))
        ys_h[c] = high
        ys_l[c] = low

    own_bc.wait()
    for d in range(1, peers):
        source = lax.rem(me + d, peers)
        bc_copy(source, source).wait_recv()
    proj_b = bcr[:, 0].reshape(tokens, -1)
    proj_c = bcr[:, 1].reshape(tokens, -1)
    bcm[0] = proj_b
    bcm[1] = proj_c
    b_t = proj_b.astype(F32).T.astype(BF16)
    c_t = proj_c.astype(F32).T.astype(BF16)
    scores_t = jnp.where(upto, dot(proj_b, proj_c, NT), 0.0)
    sm[0], sm[1] = split(scores_t)
    sm[2], sm[3] = split(scores_t.T)
    for c in range(chunks):
        pulled[c] = dot2(c_t, (ys_h[c], ys_l[c]))

    @pl.when(jnp.logical_not(has_prev))
    def _():
        state_in[...] = jnp.zeros_like(state_in)

    @pl.when(jnp.logical_not(has_next))
    def _():
        pull_in[...] = jnp.zeros_like(pull_in)

    mt_acc[...] = jnp.zeros_like(mt_acc)
    bc_acc[...] = jnp.zeros_like(bc_acc)
    dcum_acc[...] = jnp.zeros_like(dcum_acc)
    dir_acc[...] = jnp.zeros_like(dir_acc)

    own_x.wait()
    for d in range(1, peers):
        source = lax.rem(me + d, peers)
        x_copy(source, source).wait_recv()
    for c in range(chunks):
        x = xr[:, :, c * lanes : (c + 1) * lanes].reshape(tokens, lanes)
        xc[c] = x
        pair = split(ed[c] * x.astype(F32))
        xs_h[c] = pair[0]
        xs_l[c] = pair[1]
        fresh[c] = dot2(b_t, pair)

    def forward_copy(c):
        return pltpu.make_async_remote_copy(
            src_ref=state_out.at[c], dst_ref=state_in.at[c],
            send_sem=send_f.at[c], recv_sem=recv_f.at[c],
            device_id={"seq": block + 1}, device_id_type=MESH,
        )

    def backward_copy(c):
        return pltpu.make_async_remote_copy(
            src_ref=pull_out.at[c], dst_ref=pull_in.at[c],
            send_sem=send_g.at[c], recv_sem=recv_g.at[c],
            device_id={"seq": block - 1}, device_id_type=MESH,
        )

    def selector(c):
        head = lax.broadcasted_iota(jnp.int32, (HEAD_PAD, lanes), 0)
        of = lax.broadcasted_iota(jnp.int32, (HEAD_PAD, lanes), 1) // head_width
        return jnp.where(head == c * chunk_heads + of, 1.0, 0.0).astype(BF16)

    def total_decay(c):
        return ec[c, tokens - 1 : tokens, :]

    def step(s, carry):
        cf = s - SKEW * block
        cb = s - SKEW * (blocks - 1 - block)
        do_f = jnp.logical_and(cf >= 0, cf < chunks)
        do_b = jnp.logical_and(cb >= 0, cb < chunks)

        @pl.when(do_f)
        def _():
            @pl.when(has_prev)
            def _():
                forward_copy(cf).wait_recv()

            state_out[cf] = total_decay(cf) * (state_in[cf] + fresh[cf])

            @pl.when(has_next)
            def _():
                forward_copy(cf).start()

        @pl.when(do_b)
        def _():
            @pl.when(has_next)
            def _():
                backward_copy(cb).wait_recv()

            @pl.when(has_prev)
            def _():
                pull_out[cb] = total_decay(cb) * pull_in[cb] + pulled[cb]
                backward_copy(cb).start()

        @pl.when(s < chunks)
        def _():
            xs = (xs_h[s], xs_l[s])
            ys = (ys_h[s], ys_l[s])
            mt_acc[...] += dot3(xs, ys, NT)

        @pl.when(do_f)
        def _():
            entering = split(state_in[cf])
            z = joined(
                (sm[2], sm[2], sm[3], bcm[1], bcm[1]),
                (xs_h[cf], xs_l[cf], xs_h[cf], *entering),
            )
            bc_acc[1] += dot3((ys_h[cf], ys_l[cf]), entering, NT)
            v = split(ec[cf] * dyc[cf].astype(F32) * z)
            dcum_acc[...] += dot2(selector(cf), v, NT)

        @pl.when(do_b)
        def _():
            leaving = split(total_decay(cb) * pull_in[cb])
            a2 = joined(
                (sm[0], sm[0], sm[1], bcm[0], bcm[0]),
                (ys_h[cb], ys_l[cb], ys_h[cb], *leaving),
            )
            bc_acc[0] += dot3((xs_h[cb], xs_l[cb]), leaving, NT)
            x = xc[cb].astype(F32)
            growth = ed[cb]
            gx = growth * a2 + gain_row[cb, 0:1, :] * dyc[cb].astype(F32)
            gx_ref[:, pl.ds(pl.multiple_of(cb * lanes, 128), lanes)] = gx.astype(BF16)
            direct = x * a2
            pick = selector(cb)
            dir_acc[...] += dot2(pick, split(direct), NT)
            dcum_acc[...] -= dot2(pick, split(growth * direct), NT)

        return carry

    lax.fori_loop(0, chunks + SKEW * (blocks - 1), step, 0)

    inner = jnp.where(upto, mt_acc[...], 0.0)
    grad_b = bc_acc[0] + dot2l(split(inner), bcm[1])
    grad_c = bc_acc[1] + dot2l(split(inner.T), bcm[0])
    for j in range(peers):
        part[j, 0] = grad_b[j * rows : (j + 1) * rows]
        part[j, 1] = grad_c[j * rows : (j + 1) * rows]

    def sum_copy(peer, slot):
        return pltpu.make_async_remote_copy(
            src_ref=part.at[peer], dst_ref=rs.at[slot],
            send_sem=send_r.at[peer], recv_sem=recv_r.at[slot],
            device_id={"tp": peer}, device_id_type=MESH,
        )

    for d in range(1, peers):
        sum_copy(lax.rem(me + d, peers), me).start()

    edge = jnp.zeros((HEAD_PAD, 8), F32)
    for c in range(chunks):
        both = (pull_in[c] * state_out[c]).reshape(-1, 8, lanes).sum(axis=0)
        edge = edge + dot2(selector(c), split(both), NT)
    edge = jnp.sum(edge, axis=1, keepdims=True)
    after = exact(dcum_acc[...], jnp.where(row >= col, 1.0, 0.0).astype(F32)) + edge
    gstep = jnp.exp(-cums[...]) * dir_acc[...] - rates[...] * after
    gstep_ref[...] = gstep[0:head_count]

    total = part[me]
    for d in range(1, peers):
        source = lax.rem(me + d, peers)
        sum_copy(source, source).wait_recv()
        total = total + rs[source]
    gbc_ref[...] = total

    for d in range(1, peers):
        peer = lax.rem(me + d, peers)
        bc_copy(peer, me).wait_send()
        x_copy(peer, me).wait_send()
        sum_copy(peer, me).wait_send()

    def drain(c, carry):
        @pl.when(has_next)
        def _():
            forward_copy(c).wait_send()

        @pl.when(has_prev)
        def _():
            backward_copy(c).wait_send()

        return carry

    lax.fori_loop(0, chunks, drain, 0)


def shards(x_ckpt, bc_ckpt, step_sizes, decay_rate, skip_gain, grad_out):
    peers, blocks = lax.axis_size("tp"), lax.axis_size("seq")
    rows = x_ckpt.shape[0]
    head_count, tokens = step_sizes.shape
    width = grad_out.shape[1]
    state = bc_ckpt.shape[2]
    lanes = 128
    chunks = width // lanes
    head_width = width // head_count
    wide = lambda dtype, size: pltpu.VMEM((chunks, size, lanes), dtype)
    dma = lambda n: pltpu.SemaphoreType.DMA((n,))
    vmem = pl.BlockSpec(memory_space=pltpu.VMEM)
    smem = pl.BlockSpec(memory_space=pltpu.SMEM)
    heads = pltpu.VMEM((HEAD_PAD, tokens), F32)
    return pl.pallas_call(
        partial(kernel, peers, blocks, head_width),
        out_shape=(
            jax.ShapeDtypeStruct((tokens, width), BF16),
            jax.ShapeDtypeStruct((2, rows, state), F32),
            jax.ShapeDtypeStruct((head_count, tokens), F32),
        ),
        in_specs=[vmem, vmem, vmem, smem, smem, vmem],
        out_specs=(vmem, vmem, vmem),
        scratch_shapes=[
            pltpu.VMEM((peers, rows, width), BF16),
            pltpu.VMEM((peers, 2, rows, state), BF16),
            pltpu.VMEM((peers, 2, rows, state), F32),
            pltpu.VMEM((peers, 2, rows, state), F32),
            *[wide(F32, state)] * 6,
            *[wide(BF16, tokens)] * 6,
            *[wide(F32, tokens)] * 2,
            wide(F32, 8),
            heads, heads, heads, heads,
            pltpu.VMEM((tokens, tokens), F32),
            pltpu.VMEM((2, tokens, state), F32),
            heads, heads,
            pltpu.VMEM((4, tokens, tokens), BF16),
            pltpu.VMEM((2, tokens, state), BF16),
            dma(peers), dma(peers), dma(peers), dma(peers), dma(2),
            dma(chunks), dma(chunks), dma(chunks), dma(chunks),
            dma(peers), dma(peers),
        ],
        compiler_params=pltpu.CompilerParams(collective_id=0, has_side_effects=True),
    )(x_ckpt, bc_ckpt, step_sizes, decay_rate, skip_gain, grad_out)


def solution(mesh):
    return jax.shard_map(
        shards,
        mesh=mesh,
        in_specs=(
            P(("dp", "seq", "tp"), None),
            P(None, ("dp", "seq", "tp"), None),
            P("tp", ("dp", "seq")),
            P("tp"),
            P("tp"),
            P(("dp", "seq"), "tp"),
        ),
        out_specs=(
            P(("dp", "seq"), "tp"),
            P(None, ("dp", "seq", "tp"), None),
            P("tp", ("dp", "seq")),
        ),
        check_vma=False,
    )
```

profile of v0, /device:TPU:0, one launch (start us, length us, event | category | flops | bytes accessed | tf_op | source)
XLA Modules:
  0.0 43.9 jit_solution(12511298124191454889)
XLA Ops:
  0.6 40.2 %shard_map.85 = (bf16[128,1280]{1,0:T(8,128)(2,1)}, f32[2,32,128]{2,1,0:T(8,128)}, f32[20,128]{1,0:T(8,128)}) custom-call(bf16[32,5120]{1,0:T(8,128)(2,1)} %x_ref.1, bf16[2,32,128]{2,1,0:T(8,128)(2,1)} %bc_ref.1, f32[20,128]{1,0:T(8,128)} %step_ref.1, f32[20]{0:T(128)} %rate_ref.1, f32[20]{0:T(128)} %gain_ref.1, bf16[128,1280]{1,0:T(8,128)(2,1)} %dy_ref.1), custom_call_target="tpu_custom_call" | custom-call | tf_op jit(solution)/shard_map/pallas_call | solution.py:346
  40.8 0.0 copy-start
  40.8 1.7 %copy.12 = bf16[128,1280]{1,0:T(8,128)(2,1)} copy(bf16[128,1280]{1,0:T(8,128)(2,1)} %get-tuple-element.6) | data formatting | bytes 655360
  42.6 0.0 copy-done
  42.6 0.0 copy-start.1
  42.6 0.6 %copy.13 = f32[2,32,128]{2,1,0:T(8,128)} copy(f32[2,32,128]{2,1,0:T(8,128)S(1)} %copy-done) | data formatting | bytes 65536
  43.2 0.1 copy-done.1
  43.3 0.6 %copy.14 = f32[20,128]{1,0:T(8,128)} copy(f32[20,128]{1,0:T(8,128)S(1)} %copy-done.1) | data formatting | bytes 20480
Async XLA Ops:
  40.8 1.7 %copy-start = (f32[2,32,128]{2,1,0:T(8,128)S(1)}, f32[2,32,128]{2,1,0:T(8,128)}, u32[]{:S(2)}) copy-start(f32[2,32,128]{2,1,0:T(8,128)} %get-tuple-element.7) | copy-start | bytes 98308
  42.6 0.7 %copy-start.1 = (f32[20,128]{1,0:T(8,128)S(1)}, f32[20,128]{1,0:T(8,128)}, u32[]{:S(2)}) copy-start(f32[20,128]{1,0:T(8,128)} %get-tuple-element.8) | copy-start | bytes 30724
where the time goes:
time: 44.1 us; the launch traced here: 43.9 us
  Pallas kernels  40.2 us (91%)
  local copies, waits for them, and re-layouts  3.05 us (7%)
  between operations  0.65 us (1%)
    pallas_call x1, Pallas kernels, shards(): pl.pallas_call(partial(kernel, peers, blocks, head_width), out_shape=(jax...  40.2 us
    unnamed x7, local copies, waits for them, and re-layouts  3.05 us

commit v1 on v0

--- a/solution.py
+++ b/solution.py
@@ -1,3 +1,4 @@
+import math
 from functools import partial
 
 import jax
@@ -11,7 +12,8 @@
 F32 = jnp.float32
 BF16 = jnp.bfloat16
 HEAD_PAD = 32
-SKEW = 3
+SKEW = 4
+SPAN = 125.0
 
 NN = (((1,), (0,)), ((), ()))
 NT = (((1,), (1,)), ((), ()))
@@ -48,16 +50,27 @@
     return joined((a[0], a[0], a[1]), (b[0], b[1], b[0]), dims)
 
 
+def encode(v):
+    top = jnp.max(jnp.abs(v), axis=0, keepdims=True)
+    top = jnp.maximum(top, 1e-30)
+    return jnp.exp2(v * (SPAN / top)).astype(BF16), top
+
+
+def decode(code, top):
+    return jnp.log(code.astype(F32)) * (top * (1.0 / (SPAN * math.log(2.0))))
+
+
 def kernel(
     peers, blocks, head_width,
     x_ref, bc_ref, step_ref, rate_ref, gain_ref, dy_ref,
     gx_ref, gbc_ref, gstep_ref,
-    xr, bcr, part, rs,
-    state_in, state_out, pull_in, pull_out, fresh, pulled,
+    x_in, dy_in, step_in, xr, bcr, part, rs,
+    state_in, state_out, pull_in, fresh, pulled,
+    code_fo, code_fi, code_bo, code_bi, top_fo, top_fi, top_bo, top_bi,
     xs_h, xs_l, ys_h, ys_l, xc, dyc, ec, ed, gain_row,
     stp, rates, gains, cums, mt_acc, bc_acc, dcum_acc, dir_acc, sm, bcm,
     send_x, recv_x, send_b, recv_b, own_sem,
-    send_f, recv_f, send_g, recv_g, send_r, recv_r,
+    send_f, recv_f, send_g, recv_g, send_ft, recv_ft, send_gt, recv_gt, send_r, recv_r,
 ):
     me = lax.axis_index("tp")
     block = lax.axis_index("seq")
@@ -66,9 +79,25 @@
     rows = x_ref.shape[0]
     chunks, _, lanes = xc.shape
     chunk_heads = lanes // head_width
+    groups = recv_x.shape[1]
+    group_lanes = width // groups
+    group_chunks = chunks // groups
 
     has_prev = block > 0
     has_next = block < blocks - 1
+
+    own_bc = pltpu.make_async_copy(bc_ref, bcr.at[me], own_sem.at[0])
+    load_x = pltpu.make_async_copy(x_ref, x_in, own_sem.at[1])
+    own_x = pltpu.make_async_copy(
+        x_ref.at[:, pl.ds(pl.multiple_of(me * width, 128), width)], xr.at[me], own_sem.at[2]
+    )
+    load_step = pltpu.make_async_copy(step_ref, step_in, own_sem.at[3])
+    load_dy = pltpu.make_async_copy(dy_ref, dy_in, own_sem.at[4])
+    own_bc.start()
+    load_x.start()
+    load_step.start()
+    load_dy.start()
+    own_x.start()
 
     barrier = pltpu.get_barrier_semaphore()
     for d in range(1, peers):
@@ -84,37 +113,35 @@
     def _():
         pl.semaphore_signal(barrier, inc=1, device_id={"seq": block + 1}, device_id_type=MESH)
 
+    def bc_copy(peer, slot):
+        return pltpu.make_async_remote_copy(
+            src_ref=bcr.at[me], dst_ref=bcr.at[slot],
+            send_sem=send_b.at[peer], recv_sem=recv_b.at[slot],
+            device_id={"tp": peer}, device_id_type=MESH,
+        )
+
+    def x_copy(peer, slot, g):
+        start = pl.multiple_of(peer * width + g * group_lanes, 128)
+        return pltpu.make_async_remote_copy(
+            src_ref=x_in.at[:, pl.ds(start, group_lanes)],
+            dst_ref=xr.at[slot, :, pl.ds(g * group_lanes, group_lanes)],
+            send_sem=send_x.at[peer, g], recv_sem=recv_x.at[slot, g],
+            device_id={"tp": peer}, device_id_type=MESH,
+        )
+
+    own_bc.wait()
     neighbours = jnp.where(has_prev, 1, 0) + jnp.where(has_next, 1, 0)
     pl.semaphore_wait(barrier, peers - 1 + neighbours)
-
-    def bc_copy(peer, slot):
-        return pltpu.make_async_remote_copy(
-            src_ref=bc_ref, dst_ref=bcr.at[slot],
-            send_sem=send_b.at[peer], recv_sem=recv_b.at[slot],
-            device_id={"tp": peer}, device_id_type=MESH,
-        )
-
-    def x_copy(peer, slot):
-        return pltpu.make_async_remote_copy(
-            src_ref=x_ref.at[:, pl.ds(pl.multiple_of(peer * width, 128), width)],
-            dst_ref=xr.at[slot],
-            send_sem=send_x.at[peer], recv_sem=recv_x.at[slot],
-            device_id={"tp": peer}, device_id_type=MESH,
-        )
-
     for d in range(1, peers):
         bc_copy(lax.rem(me + d, peers), me).start()
-    for d in range(1, peers):
-        x_copy(lax.rem(me + d, peers), me).start()
-    own_x = pltpu.make_async_copy(
-        x_ref.at[:, pl.ds(pl.multiple_of(me * width, 128), width)], xr.at[me], own_sem.at[0]
-    )
-    own_bc = pltpu.make_async_copy(bc_ref, bcr.at[me], own_sem.at[1])
-    own_x.start()
-    own_bc.start()
-
+    load_x.wait()
+    for g in range(groups):
+        for d in range(1, peers):
+            x_copy(lax.rem(me + d, peers), me, g).start()
+
+    load_step.wait()
     stp[...] = jnp.zeros_like(stp)
-    stp[0:head_count] = step_ref[...]
+    stp[0:head_count] = step_in[...]
     rates[...] = jnp.zeros_like(rates)
     gains[...] = jnp.zeros_like(gains)
     for h in range(head_count):
@@ -131,6 +158,7 @@
     table = split(stacked.T)
     pick_row = lax.broadcasted_iota(jnp.int32, (4 * HEAD_PAD, lanes), 0)
     pick_head = lax.broadcasted_iota(jnp.int32, (4 * HEAD_PAD, lanes), 1) // head_width
+    load_dy.wait()
     for c in range(chunks):
         def spread(q):
             hit = pick_row == (q * HEAD_PAD + c * chunk_heads) + pick_head
@@ -140,13 +168,53 @@
         ec[c] = grown
         ed[c] = dot2l(table, spread(1))
         gain_row[c] = dot2l((table[0][0:16], table[1][0:16]), spread(2))[0:8]
-        dy = dy_ref[:, c * lanes : (c + 1) * lanes]
+        dy = dy_in[:, c * lanes : (c + 1) * lanes]
         dyc[c] = dy
         high, low = split(grown * dy.astype(F32))
         ys_h[c] = high
         ys_l[c] = low
 
-    own_bc.wait()
+    def forward_copies(c):
+        return (
+            pltpu.make_async_remote_copy(
+                src_ref=top_fo.at[c], dst_ref=top_fi.at[c],
+                send_sem=send_ft.at[c], recv_sem=recv_ft.at[c],
+                device_id={"seq": block + 1}, device_id_type=MESH,
+            ),
+            pltpu.make_async_remote_copy(
+                src_ref=code_fo.at[c], dst_ref=code_fi.at[c],
+                send_sem=send_f.at[c], recv_sem=recv_f.at[c],
+                device_id={"seq": block + 1}, device_id_type=MESH,
+            ),
+        )
+
+    def backward_copies(c):
+        return (
+            pltpu.make_async_remote_copy(
+                src_ref=top_bo.at[c], dst_ref=top_bi.at[c],
+                send_sem=send_gt.at[c], recv_sem=recv_gt.at[c],
+                device_id={"seq": block - 1}, device_id_type=MESH,
+            ),
+            pltpu.make_async_remote_copy(
+                src_ref=code_bo.at[c], dst_ref=code_bi.at[c],
+                send_sem=send_g.at[c], recv_sem=recv_g.at[c],
+                device_id={"seq": block - 1}, device_id_type=MESH,
+            ),
+        )
+
+    def send_forward(c, value):
+        code_fo[c], top_fo[c] = encode(value)
+        for copy in forward_copies(c):
+            copy.start()
+
+    def send_backward(c, value):
+        code_bo[c], top_bo[c] = encode(value)
+        for copy in backward_copies(c):
+            copy.start()
+
+    def total_decay(c):
+        return ec[c, tokens - 1 : tokens, :]
+
     for d in range(1, peers):
         source = lax.rem(me + d, peers)
         bc_copy(source, source).wait_recv()
@@ -154,13 +222,20 @@
     proj_c = bcr[:, 1].reshape(tokens, -1)
     bcm[0] = proj_b
     bcm[1] = proj_c
+    c_t = proj_c.astype(F32).T.astype(BF16)
+    for c in range(chunks):
+        pulled[c] = dot2(c_t, (ys_h[c], ys_l[c]))
+
+        if c % group_chunks == group_chunks - 1:
+            @pl.when(jnp.logical_and(jnp.logical_not(has_next), has_prev))
+            def _():
+                for k in range(c - group_chunks + 1, c + 1):
+                    send_backward(k, pulled[k])
+
     b_t = proj_b.astype(F32).T.astype(BF16)
-    c_t = proj_c.astype(F32).T.astype(BF16)
     scores_t = jnp.where(upto, dot(proj_b, proj_c, NT), 0.0)
     sm[0], sm[1] = split(scores_t)
     sm[2], sm[3] = split(scores_t.T)
-    for c in range(chunks):
-        pulled[c] = dot2(c_t, (ys_h[c], ys_l[c]))
 
     @pl.when(jnp.logical_not(has_prev))
     def _():
@@ -176,38 +251,32 @@
     dir_acc[...] = jnp.zeros_like(dir_acc)
 
     own_x.wait()
-    for d in range(1, peers):
-        source = lax.rem(me + d, peers)
-        x_copy(source, source).wait_recv()
-    for c in range(chunks):
-        x = xr[:, :, c * lanes : (c + 1) * lanes].reshape(tokens, lanes)
-        xc[c] = x
-        pair = split(ed[c] * x.astype(F32))
-        xs_h[c] = pair[0]
-        xs_l[c] = pair[1]
-        fresh[c] = dot2(b_t, pair)
-
-    def forward_copy(c):
-        return pltpu.make_async_remote_copy(
-            src_ref=state_out.at[c], dst_ref=state_in.at[c],
-            send_sem=send_f.at[c], recv_sem=recv_f.at[c],
-            device_id={"seq": block + 1}, device_id_type=MESH,
-        )
-
-    def backward_copy(c):
-        return pltpu.make_async_remote_copy(
-            src_ref=pull_out.at[c], dst_ref=pull_in.at[c],
-            send_sem=send_g.at[c], recv_sem=recv_g.at[c],
-            device_id={"seq": block - 1}, device_id_type=MESH,
-        )
+    for g in range(groups):
+        for d in range(1, peers):
+            source = lax.rem(me + d, peers)
+            x_copy(source, source, g).wait_recv()
+        for c in range(g * group_chunks, (g + 1) * group_chunks):
+            x = xr[:, :, c * lanes : (c + 1) * lanes].reshape(tokens, lanes)
+            xc[c] = x
+            pair = split(ed[c] * x.astype(F32))
+            xs_h[c] = pair[0]
+            xs_l[c] = pair[1]
+            fresh[c] = dot2(b_t, pair)
+
+        @pl.when(jnp.logical_not(has_prev))
+        def _():
+            for c in range(g * group_chunks, (g + 1) * group_chunks):
+                state_out[c] = total_decay(c) * fresh[c]
+
+            @pl.when(has_next)
+            def _():
+                for c in range(g * group_chunks, (g + 1) * group_chunks):
+                    send_forward(c, state_out[c])
 
     def selector(c):
         head = lax.broadcasted_iota(jnp.int32, (HEAD_PAD, lanes), 0)
         of = lax.broadcasted_iota(jnp.int32, (HEAD_PAD, lanes), 1) // head_width
         return jnp.where(head == c * chunk_heads + of, 1.0, 0.0).astype(BF16)
-
-    def total_decay(c):
-        return ec[c, tokens - 1 : tokens, :]
 
     def step(s, carry):
         cf = s - SKEW * block
@@ -215,28 +284,29 @@
         do_f = jnp.logical_and(cf >= 0, cf < chunks)
         do_b = jnp.logical_and(cb >= 0, cb < chunks)
 
-        @pl.when(do_f)
-        def _():
+        @pl.when(jnp.logical_and(do_f, has_prev))
+        def _():
+            for copy in forward_copies(cf):
+                copy.wait_recv()
+            entering = decode(code_fi[cf], top_fi[cf])
+            state_in[cf] = entering
+            leaving = total_decay(cf) * (entering + fresh[cf])
+            state_out[cf] = leaving
+
+            @pl.when(has_next)
+            def _():
+                send_forward(cf, leaving)
+
+        @pl.when(jnp.logical_and(do_b, has_next))
+        def _():
+            for copy in backward_copies(cb):
+                copy.wait_recv()
+            arriving = decode(code_bi[cb], top_bi[cb])
+            pull_in[cb] = arriving
+
             @pl.when(has_prev)
             def _():
-                forward_copy(cf).wait_recv()
-
-            state_out[cf] = total_decay(cf) * (state_in[cf] + fresh[cf])
-
-            @pl.when(has_next)
-            def _():
-                forward_copy(cf).start()
-
-        @pl.when(do_b)
-        def _():
-            @pl.when(has_next)
-            def _():
-                backward_copy(cb).wait_recv()
-
-            @pl.when(has_prev)
-            def _():
-                pull_out[cb] = total_decay(cb) * pull_in[cb] + pulled[cb]
-                backward_copy(cb).start()
+                send_backward(cb, total_decay(cb) * arriving + pulled[cb])
 
         @pl.when(s < chunks)
         def _():
@@ -312,17 +382,20 @@
     for d in range(1, peers):
         peer = lax.rem(me + d, peers)
         bc_copy(peer, me).wait_send()
-        x_copy(peer, me).wait_send()
+        for g in range(groups):
+            x_copy(peer, me, g).wait_send()
         sum_copy(peer, me).wait_send()
 
     def drain(c, carry):
         @pl.when(has_next)
         def _():
-            forward_copy(c).wait_send()
+            for copy in forward_copies(c):
+                copy.wait_send()
 
         @pl.when(has_prev)
         def _():
-            backward_copy(c).wait_send()
+            for copy in backward_copies(c):
+                copy.wait_send()
 
         return carry
 
@@ -338,26 +411,33 @@
     lanes = 128
     chunks = width // lanes
     head_width = width // head_count
+    groups = chunks // 2 if chunks % 2 == 0 else chunks
     wide = lambda dtype, size: pltpu.VMEM((chunks, size, lanes), dtype)
     dma = lambda n: pltpu.SemaphoreType.DMA((n,))
     vmem = pl.BlockSpec(memory_space=pltpu.VMEM)
+    hbm = pl.BlockSpec(memory_space=pl.ANY)
     smem = pl.BlockSpec(memory_space=pltpu.SMEM)
     heads = pltpu.VMEM((HEAD_PAD, tokens), F32)
     return pl.pallas_call(
         partial(kernel, peers, blocks, head_width),
         out_shape=(
-            jax.ShapeDtypeStruct((tokens, width), BF16),
-            jax.ShapeDtypeStruct((2, rows, state), F32),
-            jax.ShapeDtypeStruct((head_count, tokens), F32),
+            pltpu.VMEM((tokens, width), BF16),
+            pltpu.VMEM((2, rows, state), F32),
+            pltpu.VMEM((head_count, tokens), F32),
         ),
-        in_specs=[vmem, vmem, vmem, smem, smem, vmem],
+        in_specs=[hbm, hbm, hbm, smem, smem, hbm],
         out_specs=(vmem, vmem, vmem),
         scratch_shapes=[
+            pltpu.VMEM(x_ckpt.shape, BF16),
+            pltpu.VMEM((tokens, width), BF16),
+            pltpu.VMEM((head_count, tokens), F32),
             pltpu.VMEM((peers, rows, width), BF16),
             pltpu.VMEM((peers, 2, rows, state), BF16),
             pltpu.VMEM((peers, 2, rows, state), F32),
             pltpu.VMEM((peers, 2, rows, state), F32),
-            *[wide(F32, state)] * 6,
+            *[wide(F32, state)] * 5,
+            *[wide(BF16, state)] * 4,
+            *[wide(F32, 1)] * 4,
             *[wide(BF16, tokens)] * 6,
             *[wide(F32, tokens)] * 2,
             wide(F32, 8),
@@ -367,8 +447,9 @@
             heads, heads,
             pltpu.VMEM((4, tokens, tokens), BF16),
             pltpu.VMEM((2, tokens, state), BF16),
-            dma(peers), dma(peers), dma(peers), dma(peers), dma(2),
-            dma(chunks), dma(chunks), dma(chunks), dma(chunks),
+            pltpu.SemaphoreType.DMA((peers, groups)), pltpu.SemaphoreType.DMA((peers, groups)),
+            dma(peers), dma(peers), dma(5),
+            *[dma(chunks)] * 8,
             dma(peers), dma(peers),
         ],
         compiler_params=pltpu.CompilerParams(collective_id=0, has_side_effects=True),

time: 44.1 us -> 35.1 us (0.80)
  Pallas kernels: 40.2 us -> 32.2 us
  local copies, waits for them, and re-layouts: 3.05 us -> 1.94 us
    pallas_call x1, Pallas kernels: 40.2 us -> 32.2 us  [shards(): pl.pallas_call(partial(kernel, peers, blocks, head_width), out_shape=(plt...]
    unnamed x7 -> x3, local copies, waits for them, and re-layouts: 3.05 us -> 1.94 us
where the time goes in v1:
time: 35.1 us; the launch traced here: 34.8 us
  Pallas kernels  32.2 us (92%)
  local copies, waits for them, and re-layouts  1.94 us (6%)
  between operations  0.64 us (2%)
    pallas_call x1, Pallas kernels, shards(): pl.pallas_call(partial(kernel, peers, blocks, head_width), out_shape=(plt...  32.2 us
    unnamed x3, local copies, waits for them, and re-layouts  1.94 us

profile of v1, /device:TPU:0, one launch (start us, length us, event | category | flops | bytes accessed | tf_op | source)
XLA Modules:
  0.0 34.8 jit_solution(3506189732922851242)
XLA Ops:
  0.6 32.2 %shard_map.85 = (bf16[128,1280]{1,0:T(8,128)(2,1)S(1)}, f32[2,32,128]{2,1,0:T(8,128)S(1)}, f32[20,128]{1,0:T(8,128)S(1)}) custom-call(bf16[32,5120]{1,0:T(8,128)(2,1)} %x_ref.1, bf16[2,32,128]{2,1,0:T(8,128)(2,1)} %bc_ref.1, f32[20,128]{1,0:T(8,128)} %step_ref.1, f32[20]{0:T(128)} %rate_ref.1, f32[20]{0:T(128)} %gain_ref.1, bf16[128,1280]{1,0:T(8,128)(2,1)} %dy_ref.1), custom_call_target="tpu_custom_call" | custom-call | tf_op jit(solution)/shard_map/pallas_call | solution.py:421
  32.9 0.7 %copy.12 = bf16[128,1280]{1,0:T(8,128)(2,1)} copy(bf16[128,1280]{1,0:T(8,128)(2,1)S(1)} %get-tuple-element.3) | data formatting | bytes 655360
  33.6 0.6 %copy.14 = f32[20,128]{1,0:T(8,128)} copy(f32[20,128]{1,0:T(8,128)S(1)} %get-tuple-element.5) | data formatting | bytes 20480
  34.2 0.6 %copy.13 = f32[2,32,128]{2,1,0:T(8,128)} copy(f32[2,32,128]{2,1,0:T(8,128)S(1)} %get-tuple-element.4) | data formatting | bytes 65536

commit v2 on v1

v2 whole, which is shorter than its diff:
```python
import math
from functools import partial

import jax
import jax.numpy as jnp
from jax import lax
from jax.experimental import pallas as pl
from jax.experimental.pallas import tpu as pltpu
from jax.sharding import PartitionSpec as P

MESH = pl.DeviceIdType.MESH
F32 = jnp.float32
BF16 = jnp.bfloat16
HEAD_PAD = 32
SKEW = 4
SPAN = 125.0
TOP_ROWS = 8

NN = (((1,), (0,)), ((), ()))
NT = (((1,), (1,)), ((), ()))


def dot(a, b, dims=NN):
    return lax.dot_general(a, b, dims, preferred_element_type=F32)


def exact(a, b):
    return lax.dot_general(
        a, b, NN, precision=lax.Precision.HIGHEST, preferred_element_type=F32
    )


def split(v):
    high = v.astype(BF16)
    return high, (v - high.astype(F32)).astype(BF16)


def joined(a, b, dims=NN):
    return dot(jnp.concatenate(a, axis=1), jnp.concatenate(b, axis=dims[0][1][0]), dims)


def dot2(a, b, dims=NN):
    return joined((a, a), b, dims)


def dot2l(a, b, dims=NN):
    return joined(a, (b, b), dims)


def dot3(a, b, dims=NN):
    return joined((a[0], a[0], a[1]), (b[0], b[1], b[0]), dims)


def encode(v):
    top = jnp.max(jnp.abs(v), axis=0, keepdims=True)
    top = jnp.maximum(top, 1e-30).astype(BF16)
    code = jnp.exp2(v * (SPAN / top.astype(F32))).astype(BF16)
    return jnp.concatenate([code, jnp.broadcast_to(top, (TOP_ROWS, v.shape[1]))], axis=0)


def decode(message):
    size = message.shape[0] - TOP_ROWS
    top = message[size : size + 1].astype(F32)
    return jnp.log(message[0:size].astype(F32)) * (top * (1.0 / (SPAN * math.log(2.0))))


def kernel(
    peers, blocks, head_width,
    x_ref, bc_ref, step_ref, rate_ref, gain_ref, dy_ref,
    gx_ref, gbc_ref, gstep_ref,
    x_in, dy_in, step_in, xr, bcr, rs,
    state_in, state_out, pull_in, fresh, pulled,
    code_fo, code_fi, code_bo, code_bi,
    xs_h, xs_l, ys_h, ys_l, xc, dyc, ec, ed, gain_row,
    stp, rates, gains, cums, bc_acc, dcum_acc, dir_acc, sm, bcm,
    rate_sm, gain_sm, own_sem, send_sem, recv_x, recv_b, recv_f, recv_g, recv_r,
):
    me = lax.axis_index("tp")
    block = lax.axis_index("seq")
    head_count, tokens = step_ref.shape
    width = dy_ref.shape[1]
    rows = x_ref.shape[0]
    chunks, _, lanes = xc.shape
    chunk_heads = lanes // head_width
    groups = recv_x.shape[0]
    group_lanes = width // groups
    group_chunks = chunks // groups

    has_prev = block > 0
    has_next = block < blocks - 1

    barrier = pltpu.get_barrier_semaphore()
    for d in range(1, peers):
        pl.semaphore_signal(
            barrier, inc=1, device_id={"tp": lax.rem(me + d, peers)}, device_id_type=MESH
        )

    @pl.when(has_prev)
    def _():
        pl.semaphore_signal(barrier, inc=1, device_id={"seq": block - 1}, device_id_type=MESH)

    @pl.when(has_next)
    def _():
        pl.semaphore_signal(barrier, inc=1, device_id={"seq": block + 1}, device_id_type=MESH)

    own_bc = pltpu.make_async_copy(bc_ref, bcr.at[me], own_sem.at[0])
    load_x = pltpu.make_async_copy(x_ref, x_in, own_sem.at[1])
    own_x = pltpu.make_async_copy(
        x_ref.at[:, pl.ds(pl.multiple_of(me * width, 128), width)], xr.at[me], own_sem.at[2]
    )
    load_step = pltpu.make_async_copy(step_ref, step_in, own_sem.at[3])
    load_dy = pltpu.make_async_copy(dy_ref, dy_in, own_sem.at[4])
    load_rate = pltpu.make_async_copy(rate_ref, rate_sm, own_sem.at[5])
    load_gain = pltpu.make_async_copy(gain_ref, gain_sm, own_sem.at[6])
    own_bc.start()
    load_x.start()
    load_step.start()
    load_dy.start()
    own_x.start()
    load_rate.start()
    load_gain.start()

    def bc_copy(peer, slot):
        return pltpu.make_async_remote_copy(
            src_ref=bcr.at[me], dst_ref=bcr.at[slot],
            send_sem=send_sem.at[0], recv_sem=recv_b.at[0],
            device_id={"tp": peer}, device_id_type=MESH,
        )

    def x_copy(peer, slot, g):
        start = pl.multiple_of(peer * width + g * group_lanes, 128)
        return pltpu.make_async_remote_copy(
            src_ref=x_in.at[:, pl.ds(start, group_lanes)],
            dst_ref=xr.at[slot, :, pl.ds(g * group_lanes, group_lanes)],
            send_sem=send_sem.at[1], recv_sem=recv_x.at[g],
            device_id={"tp": peer}, device_id_type=MESH,
        )

    own_bc.wait()
    neighbours = jnp.where(has_prev, 1, 0) + jnp.where(has_next, 1, 0)
    pl.semaphore_wait(barrier, peers - 1 + neighbours)
    for d in range(1, peers):
        bc_copy(lax.rem(me + d, peers), me).start()
    load_x.wait()
    for g in range(groups):
        for d in range(1, peers):
            x_copy(lax.rem(me + d, peers), me, g).start()

    load_step.wait()
    load_rate.wait()
    load_gain.wait()
    stp[...] = jnp.zeros_like(stp)
    stp[0:head_count] = step_in[...]
    rates[...] = jnp.zeros_like(rates)
    gains[...] = jnp.zeros_like(gains)
    for h in range(head_count):
        rates[h : h + 1] = jnp.full((1, tokens), rate_sm[h], F32)
        gains[h : h + 1] = jnp.full((1, tokens), gain_sm[h], F32)
    row = lax.broadcasted_iota(jnp.int32, (tokens, tokens), 0)
    col = lax.broadcasted_iota(jnp.int32, (tokens, tokens), 1)
    upto = row <= col
    cum = exact(-rates[...] * stp[...], jnp.where(upto, 1.0, 0.0).astype(F32))
    cums[...] = cum
    stacked = jnp.concatenate(
        [jnp.exp(cum), jnp.exp(-cum) * stp[...], gains[...], jnp.zeros_like(cum)], axis=0
    )
    table = split(stacked.T)
    pick_row = lax.broadcasted_iota(jnp.int32, (4 * HEAD_PAD, lanes), 0)
    pick_head = lax.broadcasted_iota(jnp.int32, (4 * HEAD_PAD, lanes), 1) // head_width
    load_dy.wait()
    for c in range(chunks):
        def spread(q):
            hit = pick_row == (q * HEAD_PAD + c * chunk_heads) + pick_head
            return jnp.where(hit, 1.0, 0.0).astype(BF16)

        grown = dot2l(table, spread(0))
        ec[c] = grown
        ed[c] = dot2l(table, spread(1))
        gain_row[c] = dot2l((table[0][0:16], table[1][0:16]), spread(2))[0:8]
        dy = dy_in[:, c * lanes : (c + 1) * lanes]
        dyc[c] = dy
        high, low = split(grown * dy.astype(F32))
        ys_h[c] = high
        ys_l[c] = low

    def forward_copy(c):
        return pltpu.make_async_remote_copy(
            src_ref=code_fo.at[c], dst_ref=code_fi.at[c],
            send_sem=send_sem.at[2], recv_sem=recv_f.at[c],
            device_id={"seq": block + 1}, device_id_type=MESH,
        )

    def backward_copy(c):
        return pltpu.make_async_remote_copy(
            src_ref=code_bo.at[c], dst_ref=code_bi.at[c],
            send_sem=send_sem.at[3], recv_sem=recv_g.at[c],
            device_id={"seq": block - 1}, device_id_type=MESH,
        )

    def landing(ref, sem, slot):
        return pltpu.make_async_remote_copy(
            src_ref=ref, dst_ref=ref, send_sem=send_sem.at[slot], recv_sem=sem,
            device_id={"tp": lax.rem(me + 1, peers)}, device_id_type=MESH,
        )

    def send_forward(c, value):
        code_fo[c] = encode(value)
        forward_copy(c).start()

    def send_backward(c, value):
        code_bo[c] = encode(value)
        backward_copy(c).start()

    def total_decay(c):
        return ec[c, tokens - 1 : tokens, :]

    landing(bcr.at[pl.ds(0, peers - 1)], recv_b.at[0], 0).wait_recv()
    proj_b = bcr[:, 0].reshape(tokens, -1)
    proj_c = bcr[:, 1].reshape(tokens, -1)
    bcm[0] = proj_b
    bcm[1] = proj_c
    c_t = proj_c.astype(F32).T.astype(BF16)
    for c in range(chunks):
        pulled[c] = dot2(c_t, (ys_h[c], ys_l[c]))

        if c % group_chunks == group_chunks - 1:
            @pl.when(jnp.logical_and(jnp.logical_not(has_next), has_prev))
            def _():
                for k in range(c - group_chunks + 1, c + 1):
                    send_backward(k, pulled[k])

    b_t = proj_b.astype(F32).T.astype(BF16)
    scores_t = jnp.where(upto, dot(proj_b, proj_c, NT), 0.0)
    sm[0], sm[1] = split(scores_t)
    sm[2], sm[3] = split(scores_t.T)

    @pl.when(jnp.logical_not(has_prev))
    def _():
        state_in[...] = jnp.zeros_like(state_in)

    @pl.when(jnp.logical_not(has_next))
    def _():
        pull_in[...] = jnp.zeros_like(pull_in)

    dcum_acc[...] = jnp.zeros_like(dcum_acc)
    dir_acc[...] = jnp.zeros_like(dir_acc)

    own_x.wait()
    for g in range(groups):
        group = xr.at[pl.ds(0, peers - 1), :, pl.ds(g * group_lanes, group_lanes)]
        landing(group, recv_x.at[g], 1).wait_recv()
        for c in range(g * group_chunks, (g + 1) * group_chunks):
            x = xr[:, :, c * lanes : (c + 1) * lanes].reshape(tokens, lanes)
            xc[c] = x
            pair = split(ed[c] * x.astype(F32))
            xs_h[c] = pair[0]
            xs_l[c] = pair[1]
            fresh[c] = dot2(b_t, pair)

        @pl.when(jnp.logical_not(has_prev))
        def _():
            for c in range(g * group_chunks, (g + 1) * group_chunks):
                state_out[c] = total_decay(c) * fresh[c]

            @pl.when(has_next)
            def _():
                for c in range(g * group_chunks, (g + 1) * group_chunks):
                    send_forward(c, state_out[c])

    inner = jnp.zeros((tokens, tokens), F32)
    for c in range(chunks):
        inner += dot3((xs_h[c], xs_l[c]), (ys_h[c], ys_l[c]), NT)
    inner = jnp.where(upto, inner, 0.0)
    bc_acc[0] = dot2l(split(inner), bcm[1])
    bc_acc[1] = dot2l(split(inner.T), bcm[0])

    def sum_copy(q, peer, slot):
        return pltpu.make_async_remote_copy(
            src_ref=bc_acc.at[q, pl.ds(pl.multiple_of(peer * rows, 8), rows)],
            dst_ref=rs.at[q, slot],
            send_sem=send_sem.at[4 + q], recv_sem=recv_r.at[q],
            device_id={"tp": peer}, device_id_type=MESH,
        )

    def send_sums(q):
        for d in range(1, peers):
            sum_copy(q, lax.rem(me + d, peers), me).start()

    @pl.when(jnp.logical_not(has_prev))
    def _():
        send_sums(1)

    @pl.when(jnp.logical_not(has_next))
    def _():
        send_sums(0)

    def selector(c):
        head = lax.broadcasted_iota(jnp.int32, (HEAD_PAD, lanes), 0)
        of = lax.broadcasted_iota(jnp.int32, (HEAD_PAD, lanes), 1) // head_width
        return jnp.where(head == c * chunk_heads + of, 1.0, 0.0).astype(BF16)

    def step(s, carry):
        cf = s - SKEW * block
        cb = s - SKEW * (blocks - 1 - block)
        do_f = jnp.logical_and(cf >= 0, cf < chunks)
        do_b = jnp.logical_and(cb >= 0, cb < chunks)

        @pl.when(jnp.logical_and(do_f, has_prev))
        def _():
            forward_copy(cf).wait_recv()
            entering = decode(code_fi[cf])
            state_in[cf] = entering
            leaving = total_decay(cf) * (entering + fresh[cf])
            state_out[cf] = leaving

            @pl.when(has_next)
            def _():
                send_forward(cf, leaving)

        @pl.when(jnp.logical_and(do_b, has_next))
        def _():
            backward_copy(cb).wait_recv()
            arriving = decode(code_bi[cb])
            pull_in[cb] = arriving

            @pl.when(has_prev)
            def _():
                send_backward(cb, total_decay(cb) * arriving + pulled[cb])

        @pl.when(do_f)
        def _():
            entering = split(state_in[cf])
            z = joined(
                (sm[2], sm[2], sm[3], bcm[1], bcm[1]),
                (xs_h[cf], xs_l[cf], xs_h[cf], *entering),
            )

            @pl.when(has_prev)
            def _():
                bc_acc[1] += dot3((ys_h[cf], ys_l[cf]), entering, NT)

            v = split(ec[cf] * dyc[cf].astype(F32) * z)
            dcum_acc[...] += dot2(selector(cf), v, NT)

        @pl.when(do_b)
        def _():
            leaving = split(total_decay(cb) * pull_in[cb])
            a2 = joined(
                (sm[0], sm[0], sm[1], bcm[0], bcm[0]),
                (ys_h[cb], ys_l[cb], ys_h[cb], *leaving),
            )

            @pl.when(has_next)
            def _():
                bc_acc[0] += dot3((xs_h[cb], xs_l[cb]), leaving, NT)

            x = xc[cb].astype(F32)
            growth = ed[cb]
            gx = growth * a2 + gain_row[cb, 0:1, :] * dyc[cb].astype(F32)
            gx_ref[:, pl.ds(pl.multiple_of(cb * lanes, 128), lanes)] = gx.astype(BF16)
            direct = x * a2
            pick = selector(cb)
            dir_acc[...] += dot2(pick, split(direct), NT)
            dcum_acc[...] -= dot2(pick, split(growth * direct), NT)

        return carry

    lax.fori_loop(0, chunks + SKEW * (blocks - 1), step, 0)

    @pl.when(has_prev)
    def _():
        send_sums(1)

    @pl.when(has_next)
    def _():
        send_sums(0)

    edge = jnp.zeros((HEAD_PAD, 8), F32)
    for c in range(chunks):
        both = (pull_in[c] * state_out[c]).reshape(-1, 8, lanes).sum(axis=0)
        edge = edge + dot2(selector(c), split(both), NT)
    edge = jnp.sum(edge, axis=1, keepdims=True)
    after = exact(dcum_acc[...], jnp.where(row >= col, 1.0, 0.0).astype(F32)) + edge
    gstep = jnp.exp(-cums[...]) * dir_acc[...] - rates[...] * after
    gstep_ref[...] = gstep[0:head_count]

    for q in range(2):
        landing(rs.at[q, pl.ds(0, peers - 1)], recv_r.at[q], 4 + q).wait_recv()
        total = bc_acc[q, pl.ds(pl.multiple_of(me * rows, 8), rows)]
        for d in range(1, peers):
            total = total + rs[q, lax.rem(me + d, peers)]
        gbc_ref[q] = total

    landing(bcr.at[pl.ds(0, peers - 1)], recv_b.at[0], 0).wait_send()
    landing(xr.at[pl.ds(0, peers - 1)], recv_x.at[0], 1).wait_send()
    for q in range(2):
        landing(rs.at[q, pl.ds(0, peers - 1)], recv_r.at[q], 4 + q).wait_send()

    @pl.when(has_next)
    def _():
        landing(code_fo, recv_f.at[0], 2).wait_send()

    @pl.when(has_prev)
    def _():
        landing(code_bo, recv_g.at[0], 3).wait_send()


def store(gx_ref, gbc_ref, gstep_ref, gx_out, gbc_out, gstep_out, sems):
    copies = [
        pltpu.make_async_copy(source, target, sems.at[k])
        for k, (source, target) in enumerate(
            ((gx_ref, gx_out), (gbc_ref, gbc_out), (gstep_ref, gstep_out))
        )
    ]
    for copy in copies:
        copy.start()
    for copy in copies:
        copy.wait()


def shards(x_ckpt, bc_ckpt, step_sizes, decay_rate, skip_gain, grad_out):
    peers, blocks = lax.axis_size("tp"), lax.axis_size("seq")
    rows = x_ckpt.shape[0]
    head_count, tokens = step_sizes.shape
    width = grad_out.shape[1]
    state = bc_ckpt.shape[2]
    lanes = 128
    chunks = width // lanes
    head_width = width // head_count
    groups = chunks // 2 if chunks % 2 == 0 else chunks
    wide = lambda dtype, size: pltpu.VMEM((chunks, size, lanes), dtype)
    dma = lambda n: pltpu.SemaphoreType.DMA((n,))
    vmem = pl.BlockSpec(memory_space=pltpu.VMEM)
    hbm = pl.BlockSpec(memory_space=pl.ANY)
    heads = pltpu.VMEM((HEAD_PAD, tokens), F32)
    outs = (
        ((tokens, width), BF16),
        ((2, rows, state), F32),
        ((head_count, tokens), F32),
    )
    grads = pl.pallas_call(
        partial(kernel, peers, blocks, head_width),
        out_shape=tuple(pltpu.VMEM(shape, dtype) for shape, dtype in outs),
        in_specs=[hbm] * 6,
        out_specs=(vmem, vmem, vmem),
        scratch_shapes=[
            pltpu.VMEM(x_ckpt.shape, BF16),
            pltpu.VMEM((tokens, width), BF16),
            pltpu.VMEM((head_count, tokens), F32),
            pltpu.VMEM((peers, rows, width), BF16),
            pltpu.VMEM((peers, 2, rows, state), BF16),
            pltpu.VMEM((2, peers, rows, state), F32),
            *[wide(F32, state)] * 5,
            *[wide(BF16, state + TOP_ROWS)] * 4,
            *[wide(BF16, tokens)] * 6,
            *[wide(F32, tokens)] * 2,
            wide(F32, 8),
            heads, heads, heads, heads,
            pltpu.VMEM((2, tokens, state), F32),
            heads, heads,
            pltpu.VMEM((4, tokens, tokens), BF16),
            pltpu.VMEM((2, tokens, state), BF16),
            pltpu.SMEM((head_count,), F32), pltpu.SMEM((head_count,), F32),
            dma(7), dma(6), dma(groups), dma(1), dma(chunks), dma(chunks), dma(2),
        ],
        compiler_params=pltpu.CompilerParams(collective_id=0, has_side_effects=True),
    )(x_ckpt, bc_ckpt, step_sizes, decay_rate, skip_gain, grad_out)
    return pl.pallas_call(
        store,
        out_shape=tuple(jax.ShapeDtypeStruct(shape, dtype) for shape, dtype in outs),
        in_specs=[vmem] * 3,
        out_specs=(hbm,) * 3,
        scratch_shapes=[dma(3)],
    )(*[pltpu.with_memory_space_constraint(grad, pltpu.VMEM) for grad in grads])


def solution(mesh):
    return jax.shard_map(
        shards,
        mesh=mesh,
        in_specs=(
            P(("dp", "seq", "tp"), None),
            P(None, ("dp", "seq", "tp"), None),
            P("tp", ("dp", "seq")),
            P("tp"),
            P("tp"),
            P(("dp", "seq"), "tp"),
        ),
        out_specs=(
            P(("dp", "seq"), "tp"),
            P(None, ("dp", "seq", "tp"), None),
            P("tp", ("dp", "seq")),
        ),
        check_vma=False,
    )
```

time: 35.1 us -> 33.3 us (0.949)
  local copies, waits for them, and re-layouts: 1.94 us -> 0 us
    unnamed x3 -> x0, local copies, waits for them, and re-layouts: 1.94 us -> none
    pallas_call x1 -> x2, Pallas kernels: 32.2 us -> 32.4 us  [the longest x1 31.6 us: shards(): pl.pallas_call(partial(kernel, peers, blocks, head_width), out_shape=tupl...]
where the time goes in v2:
time: 33.3 us; the launch traced here: 33 us
  Pallas kernels  32.4 us (97%)
  between operations  0.64 us (2%)
    pallas_call x1, Pallas kernels, shards(): pl.pallas_call(partial(kernel, peers, blocks, head_width), out_shape=tupl...  31.6 us
    pallas_call x1, Pallas kernels, shards(): pl.pallas_call(store, out_shape=tuple((jax.ShapeDtypeStruct(shape, dtype)...  0.76 us

profile of v2, /device:TPU:0, one launch (start us, length us, event | category | flops | bytes accessed | tf_op | source)
XLA Modules:
  0.0 33.0 jit_solution(2187317276104013364)
XLA Ops:
  0.6 31.6 %shard_map.85 = (bf16[128,1280]{1,0:T(8,128)(2,1)S(1)}, f32[2,32,128]{2,1,0:T(8,128)S(1)}, f32[20,128]{1,0:T(8,128)S(1)}) custom-call(bf16[32,5120]{1,0:T(8,128)(2,1)} %x_ref.1, bf16[2,32,128]{2,1,0:T(8,128)(2,1)} %bc_ref.1, f32[20,128]{1,0:T(8,128)} %step_ref.1, f32[20]{0:T(128)} %rate_ref.1, f32[20]{0:T(128)} %gain_ref.1, bf16[128,1280]{1,0:T(8,128)(2,1)} %dy_ref.1), custom_call_target="tpu_custom_call" | custom-call | tf_op jit(solution)/shard_map/pallas_call | solution.py:441
  32.3 0.8 %shard_map.86 = (bf16[128,1280]{1,0:T(8,128)(2,1)}, f32[2,32,128]{2,1,0:T(8,128)}, f32[20,128]{1,0:T(8,128)}) custom-call(bf16[128,1280]{1,0:T(8,128)(2,1)S(1)} %get-tuple-element.6.gx_ref, f32[2,32,128]{2,1,0:T(8,128)S(1)} %get-tuple-element.7.gbc_ref, f32[20,128]{1,0:T(8,128)S(1)} %get-tuple-element.8.gstep_ref), custom_call_target="tpu_custom_call" | custom-call | tf_op jit(solution)/shard_map/pallas_call | solution.py:468

commit v3 on v2

--- a/solution.py
+++ b/solution.py
@@ -13,6 +13,8 @@
 BF16 = jnp.bfloat16
 HEAD_PAD = 32
 SKEW = 4
+LAG = 2
+EARLY = 2
 SPAN = 125.0
 TOP_ROWS = 8
 
@@ -71,9 +73,10 @@
     x_in, dy_in, step_in, xr, bcr, rs,
     state_in, state_out, pull_in, fresh, pulled,
     code_fo, code_fi, code_bo, code_bi,
+    near_x, near_b, near_step, next_dy, next_c, next_step, pads, weights, sides,
     xs_h, xs_l, ys_h, ys_l, xc, dyc, ec, ed, gain_row,
     stp, rates, gains, cums, bc_acc, dcum_acc, dir_acc, sm, bcm,
-    rate_sm, gain_sm, own_sem, send_sem, recv_x, recv_b, recv_f, recv_g, recv_r,
+    rate_sm, gain_sm, own_sem, send_sem, recv_x, recv_b, recv_f, recv_g, recv_r, recv_n,
 ):
     me = lax.axis_index("tp")
     block = lax.axis_index("seq")
@@ -102,6 +105,8 @@
     @pl.when(has_next)
     def _():
         pl.semaphore_signal(barrier, inc=1, device_id={"seq": block + 1}, device_id_type=MESH)
+
+    neighbours = jnp.where(has_prev, 1, 0) + jnp.where(has_next, 1, 0)
 
     own_bc = pltpu.make_async_copy(bc_ref, bcr.at[me], own_sem.at[0])
     load_x = pltpu.make_async_copy(x_ref, x_in, own_sem.at[1])
@@ -137,16 +142,48 @@
         )
 
     own_bc.wait()
-    neighbours = jnp.where(has_prev, 1, 0) + jnp.where(has_next, 1, 0)
     pl.semaphore_wait(barrier, peers - 1 + neighbours)
     for d in range(1, peers):
         bc_copy(lax.rem(me + d, peers), me).start()
+
+    early = min(EARLY, groups)
+
+    def lend(source, target, slot, sem, there):
+        return pltpu.make_async_remote_copy(
+            src_ref=source, dst_ref=target, send_sem=send_sem.at[slot], recv_sem=sem,
+            device_id={"seq": there}, device_id_type=MESH,
+        )
+
+    def group_of(g):
+        return pl.ds(pl.multiple_of(g * group_lanes, 128), group_lanes)
+
+    def lend_x(g):
+        part = (slice(None), slice(None), group_of(g))
+        return lend(xr.at[part], near_x.at[part], 7, recv_f.at[g * group_chunks], block + 1)
+
+    def lend_dy(g):
+        part = (slice(None), group_of(g))
+        return lend(dy_in.at[part], next_dy.at[part], 8, recv_g.at[g * group_chunks], block - 1)
+
+    load_step.wait()
+
+    @pl.when(block == 0)
+    def _():
+        lend(step_in, near_step, 9, recv_n.at[2], block + 1).start()
+
+    load_dy.wait()
+
+    @pl.when(block == blocks - 1)
+    def _():
+        lend(step_in, next_step, 10, recv_n.at[3], block - 1).start()
+        for g in range(early):
+            lend_dy(g).start()
+
     load_x.wait()
     for g in range(groups):
         for d in range(1, peers):
             x_copy(lax.rem(me + d, peers), me, g).start()
 
-    load_step.wait()
     load_rate.wait()
     load_gain.wait()
     stp[...] = jnp.zeros_like(stp)
@@ -167,16 +204,16 @@
     table = split(stacked.T)
     pick_row = lax.broadcasted_iota(jnp.int32, (4 * HEAD_PAD, lanes), 0)
     pick_head = lax.broadcasted_iota(jnp.int32, (4 * HEAD_PAD, lanes), 1) // head_width
-    load_dy.wait()
+
+    def spread(c, q):
+        hit = pick_row == (q * HEAD_PAD + c * chunk_heads) + pick_head
+        return jnp.where(hit, 1.0, 0.0).astype(BF16)
+
     for c in range(chunks):
-        def spread(q):
-            hit = pick_row == (q * HEAD_PAD + c * chunk_heads) + pick_head
-            return jnp.where(hit, 1.0, 0.0).astype(BF16)
-
-        grown = dot2l(table, spread(0))
+        grown = dot2l(table, spread(c, 0))
         ec[c] = grown
-        ed[c] = dot2l(table, spread(1))
-        gain_row[c] = dot2l((table[0][0:16], table[1][0:16]), spread(2))[0:8]
+        ed[c] = dot2l(table, spread(c, 1))
+        gain_row[c] = dot2l((table[0][0:16], table[1][0:16]), spread(c, 2))[0:8]
         dy = dy_in[:, c * lanes : (c + 1) * lanes]
         dyc[c] = dy
         high, low = split(grown * dy.astype(F32))
@@ -214,7 +251,39 @@
     def total_decay(c):
         return ec[c, tokens - 1 : tokens, :]
 
+    def borrow(k, steps, weigh):
+        landing(steps, recv_n.at[2 + k], 0).wait_recv()
+        pads[k] = jnp.zeros_like(pads[k])
+        pads[k, 0:head_count] = steps[...]
+        cum = exact(-rates[...] * pads[k], jnp.where(upto, 1.0, 0.0).astype(F32))
+        filler = jnp.zeros((3 * HEAD_PAD, tokens), F32)
+        table = split(jnp.concatenate([weigh(cum, pads[k]), filler], axis=0).T)
+        for c in range(chunks):
+            weights[k, c] = dot2l(table, spread(c, 0))
+
+    @pl.when(block == 1)
+    def _():
+        borrow(
+            0, near_step,
+            lambda cum, steps: jnp.exp(cum[:, tokens - 1 : tokens] - cum) * steps,
+        )
+
+    @pl.when(block == blocks - 2)
+    def _():
+        borrow(1, next_step, lambda cum, steps: jnp.exp(cum))
+
     landing(bcr.at[pl.ds(0, peers - 1)], recv_b.at[0], 0).wait_recv()
+
+    @pl.when(block == 0)
+    def _():
+        lend(bcr.at[:, 0], near_b, 6, recv_n.at[0], block + 1).start()
+
+    @pl.when(block == blocks - 1)
+    def _():
+        lend(bcr.at[:, 1], next_c, 11, recv_n.at[1], block - 1).start()
+        for g in range(early, groups):
+            lend_dy(g).start()
+
     proj_b = bcr[:, 0].reshape(tokens, -1)
     proj_c = bcr[:, 1].reshape(tokens, -1)
     bcm[0] = proj_b
@@ -223,21 +292,11 @@
     for c in range(chunks):
         pulled[c] = dot2(c_t, (ys_h[c], ys_l[c]))
 
-        if c % group_chunks == group_chunks - 1:
-            @pl.when(jnp.logical_and(jnp.logical_not(has_next), has_prev))
-            def _():
-                for k in range(c - group_chunks + 1, c + 1):
-                    send_backward(k, pulled[k])
-
     b_t = proj_b.astype(F32).T.astype(BF16)
     scores_t = jnp.where(upto, dot(proj_b, proj_c, NT), 0.0)
     sm[0], sm[1] = split(scores_t)
     sm[2], sm[3] = split(scores_t.T)
 
-    @pl.when(jnp.logical_not(has_prev))
-    def _():
-        state_in[...] = jnp.zeros_like(state_in)
-
     @pl.when(jnp.logical_not(has_next))
     def _():
         pull_in[...] = jnp.zeros_like(pull_in)
@@ -249,6 +308,11 @@
     for g in range(groups):
         group = xr.at[pl.ds(0, peers - 1), :, pl.ds(g * group_lanes, group_lanes)]
         landing(group, recv_x.at[g], 1).wait_recv()
+
+        @pl.when(block == 0)
+        def _():
+            lend_x(g).start()
+
         for c in range(g * group_chunks, (g + 1) * group_chunks):
             x = xr[:, :, c * lanes : (c + 1) * lanes].reshape(tokens, lanes)
             xc[c] = x
@@ -257,22 +321,15 @@
             xs_l[c] = pair[1]
             fresh[c] = dot2(b_t, pair)
 
-        @pl.when(jnp.logical_not(has_prev))
-        def _():
-            for c in range(g * group_chunks, (g + 1) * group_chunks):
-                state_out[c] = total_decay(c) * fresh[c]
-
-            @pl.when(has_next)
-            def _():
-                for c in range(g * group_chunks, (g + 1) * group_chunks):
-                    send_forward(c, state_out[c])
-
-    inner = jnp.zeros((tokens, tokens), F32)
-    for c in range(chunks):
-        inner += dot3((xs_h[c], xs_l[c]), (ys_h[c], ys_l[c]), NT)
-    inner = jnp.where(upto, inner, 0.0)
-    bc_acc[0] = dot2l(split(inner), bcm[1])
-    bc_acc[1] = dot2l(split(inner.T), bcm[0])
+    def finish_inner():
+        inner = jnp.zeros((tokens, tokens), F32)
+        for c in range(chunks):
+            inner += dot3((xs_h[c], xs_l[c]), (ys_h[c], ys_l[c]), NT)
+        inner = jnp.where(upto, inner, 0.0)
+        bc_acc[0] += dot2l(split(inner), bcm[1])
+        bc_acc[1] += dot2l(split(inner.T), bcm[0])
+
+    bc_acc[...] = jnp.zeros_like(bc_acc)
 
     def sum_copy(q, peer, slot):
         return pltpu.make_async_remote_copy(
@@ -286,94 +343,196 @@
         for d in range(1, peers):
             sum_copy(q, lax.rem(me + d, peers), me).start()
 
-    @pl.when(jnp.logical_not(has_prev))
-    def _():
-        send_sums(1)
-
-    @pl.when(jnp.logical_not(has_next))
-    def _():
-        send_sums(0)
-
     def selector(c):
         head = lax.broadcasted_iota(jnp.int32, (HEAD_PAD, lanes), 0)
         of = lax.broadcasted_iota(jnp.int32, (HEAD_PAD, lanes), 1) // head_width
         return jnp.where(head == c * chunk_heads + of, 1.0, 0.0).astype(BF16)
 
-    def step(s, carry):
-        cf = s - SKEW * block
-        cb = s - SKEW * (blocks - 1 - block)
-        do_f = jnp.logical_and(cf >= 0, cf < chunks)
-        do_b = jnp.logical_and(cb >= 0, cb < chunks)
-
-        @pl.when(jnp.logical_and(do_f, has_prev))
+    def rebuilt(k, c, values):
+        return dot2(sides[k], split(weights[k, c] * values.astype(F32)))
+
+    def part_of(c):
+        return pl.ds(pl.multiple_of(c * lanes, 128), lanes)
+
+    def forward_input(kind, c, opens):
+        if kind == "raw":
+            if opens:
+                group = near_x.at[:, :, pl.ds(0, group_lanes)]
+                landing(group, recv_f.at[c], 0).wait_recv()
+            entering = rebuilt(0, c, near_x[:, :, part_of(c)].reshape(tokens, lanes))
+        else:
+            forward_copy(c).wait_recv()
+            entering = decode(code_fi[c])
+        state_in[c] = entering
+        return entering
+
+    def backward_input(kind, c, opens):
+        if kind == "raw":
+            if opens:
+                landing(next_dy.at[:, pl.ds(0, group_lanes)], recv_g.at[c], 0).wait_recv()
+            arriving = rebuilt(1, c, next_dy[:, part_of(c)])
+        else:
+            backward_copy(c).wait_recv()
+            arriving = decode(code_bi[c])
+        pull_in[c] = arriving
+        return arriving
+
+    def forward_link(kind, sends, c, opens):
+        if kind == "none":
+            state_out[c] = total_decay(c) * fresh[c]
+            return
+        leaving = total_decay(c) * (forward_input(kind, c, opens) + fresh[c])
+        state_out[c] = leaving
+        if sends:
+            send_forward(c, leaving)
+
+    def backward_link(kind, sends, c, opens):
+        if kind == "none":
+            return
+        arriving = backward_input(kind, c, opens)
+        if sends:
+            send_backward(c, total_decay(c) * arriving + pulled[c])
+
+    def forward_sum(kind, c):
+        if kind != "none":
+            bc_acc[1] += dot3((ys_h[c], ys_l[c]), split(state_in[c]), NT)
+
+    def backward_sum(kind, c):
+        if kind != "none":
+            leaving = split(total_decay(c) * pull_in[c])
+            bc_acc[0] += dot3((xs_h[c], xs_l[c]), leaving, NT)
+
+    def forward_work(kind, c):
+        left, right = (sm[2], sm[2], sm[3]), (xs_h[c], xs_l[c], xs_h[c])
+        if kind != "none":
+            left, right = (*left, bcm[1], bcm[1]), (*right, *split(state_in[c]))
+        z = joined(left, right)
+        v = split(ec[c] * dyc[c].astype(F32) * z)
+        dcum_acc[...] += dot2(selector(c), v, NT)
+
+    def backward_work(kind, c):
+        left, right = (sm[0], sm[0], sm[1]), (ys_h[c], ys_l[c], ys_h[c])
+        if kind != "none":
+            leaving = split(total_decay(c) * pull_in[c])
+            left, right = (*left, bcm[0], bcm[0]), (*right, *leaving)
+        a2 = joined(left, right)
+        x = xc[c].astype(F32)
+        growth = ed[c]
+        gx = growth * a2 + gain_row[c, 0:1, :] * dyc[c].astype(F32)
+        gx_ref[:, part_of(c)] = gx.astype(BF16)
+        direct = x * a2
+        pick = selector(c)
+        dir_acc[...] += dot2(pick, split(direct), NT)
+        dcum_acc[...] -= dot2(pick, split(growth * direct), NT)
+
+    def grouped(part, *fixed):
+        def run(g):
+            for i in range(group_chunks):
+                part(*fixed, g * group_chunks + i)
+        return run
+
+    def grouped_link(part, kind, sends):
+        def run(g):
+            for i in range(group_chunks):
+                part(kind, sends, g * group_chunks + i, i == 0)
+        return run
+
+    def loop(low, high, *parts):
+        def body(k, carry):
+            for part, shift in parts:
+                part(k + shift)
+            return carry
+
+        if high > low:
+            lax.fori_loop(low, high, body, 0)
+
+    def edge_role(links, sums, work, other_work, early, late):
+        finish_inner()
+        send_sums(early)
+        loop(0, groups, (other_work, 0))
+        loop(0, groups - 1, (links, 0), (sums, 0), (work, 0))
+        links(groups - 1)
+        sums(groups - 1)
+        send_sums(late)
+        work(groups - 1)
+
+    def inner_role(lead, follow, lag):
+        (link1, sum1, work1), (link2, sum2, work2) = lead, follow
+        ahead = min(lag, groups)
+        rest = groups - ahead
+        both = min(ahead, rest)
+        loop(0, ahead, (link1, 0), (sum1, 0), (work1, 0))
+        loop(ahead, groups, (link1, 0), (link2, -ahead))
+        loop(
+            rest, rest + both, (link2, 0), (sum1, ahead - rest), (work1, ahead - rest),
+            (sum2, -rest), (work2, -rest),
+        )
+        loop(rest + both, groups, (link2, 0), (sum2, -rest), (work2, -rest))
+        loop(ahead + both, groups, (sum1, 0))
+        loop(ahead, groups, (sum2, 0))
+        finish_inner()
+        send_sums(0)
+        send_sums(1)
+        loop(ahead + both, groups, (work1, 0))
+        loop(ahead, groups, (work2, 0))
+
+    def between(s, carry):
+        cf = s - SKEW * (block - 1)
+        cb = s - SKEW * (blocks - 2 - block)
+
+        @pl.when(jnp.logical_and(cf >= 0, cf < chunks))
         def _():
-            forward_copy(cf).wait_recv()
-            entering = decode(code_fi[cf])
-            state_in[cf] = entering
-            leaving = total_decay(cf) * (entering + fresh[cf])
-            state_out[cf] = leaving
-
-            @pl.when(has_next)
-            def _():
-                send_forward(cf, leaving)
-
-        @pl.when(jnp.logical_and(do_b, has_next))
+            forward_link("code", True, cf, True)
+            forward_sum("code", cf)
+            forward_work("code", cf)
+
+        @pl.when(jnp.logical_and(cb >= 0, cb < chunks))
         def _():
-            backward_copy(cb).wait_recv()
-            arriving = decode(code_bi[cb])
-            pull_in[cb] = arriving
-
-            @pl.when(has_prev)
-            def _():
-                send_backward(cb, total_decay(cb) * arriving + pulled[cb])
-
-        @pl.when(do_f)
+            backward_link("code", True, cb, True)
+            backward_sum("code", cb)
+            backward_work("code", cb)
+
+        return carry
+
+    special = sorted({0, 1, blocks - 2, blocks - 1})
+    for b in special:
+        @pl.when(block == b)
         def _():
-            entering = split(state_in[cf])
-            z = joined(
-                (sm[2], sm[2], sm[3], bcm[1], bcm[1]),
-                (xs_h[cf], xs_l[cf], xs_h[cf], *entering),
+            forward = "none" if b == 0 else "raw" if b == 1 else "code"
+            backward = "none" if b == blocks - 1 else "raw" if b == blocks - 2 else "code"
+            if forward == "raw":
+                landing(near_b, recv_n.at[0], 0).wait_recv()
+                sides[0] = near_b[...].reshape(tokens, -1).astype(F32).T.astype(BF16)
+            if backward == "raw":
+                landing(next_c, recv_n.at[1], 0).wait_recv()
+                sides[1] = next_c[...].reshape(tokens, -1).astype(F32).T.astype(BF16)
+            sends = forward != "none" and backward != "none"
+            ahead = (
+                grouped_link(forward_link, forward, sends),
+                grouped(forward_sum, forward), grouped(forward_work, forward),
             )
-
-            @pl.when(has_prev)
-            def _():
-                bc_acc[1] += dot3((ys_h[cf], ys_l[cf]), entering, NT)
-
-            v = split(ec[cf] * dyc[cf].astype(F32) * z)
-            dcum_acc[...] += dot2(selector(cf), v, NT)
-
-        @pl.when(do_b)
+            behind = (
+                grouped_link(backward_link, backward, sends),
+                grouped(backward_sum, backward), grouped(backward_work, backward),
+            )
+            if forward == "none":
+                loop(0, groups, (ahead[0], 0))
+                edge_role(*behind, ahead[2], 1, 0)
+            elif backward == "none":
+                edge_role(*ahead, behind[2], 0, 1)
+            else:
+                lag = LAG * ((blocks - 2 - b) - (b - 1))
+                if lag < 0:
+                    ahead, behind = behind, ahead
+                inner_role(ahead, behind, abs(lag))
+
+    if blocks > 4:
+        @pl.when(jnp.logical_and(block > 1, block < blocks - 2))
         def _():
-            leaving = split(total_decay(cb) * pull_in[cb])
-            a2 = joined(
-                (sm[0], sm[0], sm[1], bcm[0], bcm[0]),
-                (ys_h[cb], ys_l[cb], ys_h[cb], *leaving),
-            )
-
-            @pl.when(has_next)
-            def _():
-                bc_acc[0] += dot3((xs_h[cb], xs_l[cb]), leaving, NT)
-
-            x = xc[cb].astype(F32)
-            growth = ed[cb]
-            gx = growth * a2 + gain_row[cb, 0:1, :] * dyc[cb].astype(F32)
-            gx_ref[:, pl.ds(pl.multiple_of(cb * lanes, 128), lanes)] = gx.astype(BF16)
-            direct = x * a2
-            pick = selector(cb)
-            dir_acc[...] += dot2(pick, split(direct), NT)
-            dcum_acc[...] -= dot2(pick, split(growth * direct), NT)
-
-        return carry
-
-    lax.fori_loop(0, chunks + SKEW * (blocks - 1), step, 0)
-
-    @pl.when(has_prev)
-    def _():
-        send_sums(1)
-
-    @pl.when(has_next)
-    def _():
-        send_sums(0)
+            lax.fori_loop(0, chunks + SKEW * (blocks - 3), between, 0)
+            finish_inner()
+            send_sums(1)
+            send_sums(0)
 
     edge = jnp.zeros((HEAD_PAD, 8), F32)
     for c in range(chunks):
@@ -396,13 +555,24 @@
     for q in range(2):
         landing(rs.at[q, pl.ds(0, peers - 1)], recv_r.at[q], 4 + q).wait_send()
 
-    @pl.when(has_next)
+    inner_block = jnp.logical_and(has_prev, has_next)
+
+    @pl.when(inner_block)
     def _():
         landing(code_fo, recv_f.at[0], 2).wait_send()
-
-    @pl.when(has_prev)
-    def _():
         landing(code_bo, recv_g.at[0], 3).wait_send()
+
+    @pl.when(block == 0)
+    def _():
+        landing(near_b, recv_n.at[0], 6).wait_send()
+        landing(near_step, recv_n.at[2], 9).wait_send()
+        landing(near_x, recv_f.at[0], 7).wait_send()
+
+    @pl.when(block == blocks - 1)
+    def _():
+        landing(next_c, recv_n.at[1], 11).wait_send()
+        landing(next_step, recv_n.at[3], 10).wait_send()
+        landing(dy_in, recv_g.at[0], 8).wait_send()
 
 
 def store(gx_ref, gbc_ref, gstep_ref, gx_out, gbc_out, gstep_out, sems):
@@ -452,6 +622,15 @@
             pltpu.VMEM((2, peers, rows, state), F32),
             *[wide(F32, state)] * 5,
             *[wide(BF16, state + TOP_ROWS)] * 4,
+            pltpu.VMEM((peers, rows, width), BF16),
+            pltpu.VMEM((peers, rows, state), BF16),
+            pltpu.VMEM((head_count, tokens), F32),
+            pltpu.VMEM((tokens, width), BF16),
+            pltpu.VMEM((peers, rows, state), BF16),
+            pltpu.VMEM((head_count, tokens), F32),
+            pltpu.VMEM((2, HEAD_PAD, tokens), F32),
+            pltpu.VMEM((2, chunks, tokens, lanes), F32),
+            pltpu.VMEM((2, state, tokens), BF16),
             *[wide(BF16, tokens)] * 6,
             *[wide(F32, tokens)] * 2,
             wide(F32, 8),
@@ -461,7 +640,7 @@
             pltpu.VMEM((4, tokens, tokens), BF16),
             pltpu.VMEM((2, tokens, state), BF16),
             pltpu.SMEM((head_count,), F32), pltpu.SMEM((head_count,), F32),
-            dma(7), dma(6), dma(groups), dma(1), dma(chunks), dma(chunks), dma(2),
+            dma(7), dma(12), dma(groups), dma(1), dma(chunks), dma(chunks), dma(2), dma(4),
         ],
         compiler_params=pltpu.CompilerParams(collective_id=0, has_side_effects=True),
     )(x_ckpt, bc_ckpt, step_sizes, decay_rate, skip_gain, grad_out)

time: 33.3 us -> 30 us (0.901)
  Pallas kernels: 32.4 us -> 29.1 us
    pallas_call x1, Pallas kernels: 31.6 us -> 28.3 us  [shards(): pl.pallas_call(partial(kernel, peers, blocks, head_width), out_shape=tupl...]
where the time goes in v3:
time: 30 us; the launch traced here: 29.7 us
  Pallas kernels  29.1 us (97%)
  between operations  0.64 us (2%)
    pallas_call x1, Pallas kernels, shards(): pl.pallas_call(partial(kernel, peers, blocks, head_width), out_shape=tupl...  28.3 us
    pallas_call x1, Pallas kernels, shards(): pl.pallas_call(store, out_shape=tuple((jax.ShapeDtypeStruct(shape, dtype)...  0.76 us

profile of v3, /device:TPU:0, one launch (start us, length us, event | category | flops | bytes accessed | tf_op | source)
XLA Modules:
  0.0 29.7 jit_solution(7882273052597199462)
XLA Ops:
  0.6 28.3 %shard_map.85 = (bf16[128,1280]{1,0:T(8,128)(2,1)S(1)}, f32[2,32,128]{2,1,0:T(8,128)S(1)}, f32[20,128]{1,0:T(8,128)S(1)}) custom-call(bf16[32,5120]{1,0:T(8,128)(2,1)} %x_ref.1, bf16[2,32,128]{2,1,0:T(8,128)(2,1)} %bc_ref.1, f32[20,128]{1,0:T(8,128)} %step_ref.1, f32[20]{0:T(128)} %rate_ref.1, f32[20]{0:T(128)} %gain_ref.1, bf16[128,1280]{1,0:T(8,128)(2,1)} %dy_ref.1), custom_call_target="tpu_custom_call" | custom-call | tf_op jit(solution)/shard_map/pallas_call | solution.py:611
  29.0 0.8 %shard_map.86 = (bf16[128,1280]{1,0:T(8,128)(2,1)}, f32[2,32,128]{2,1,0:T(8,128)}, f32[20,128]{1,0:T(8,128)}) custom-call(bf16[128,1280]{1,0:T(8,128)(2,1)S(1)} %get-tuple-element.6.gx_ref, f32[2,32,128]{2,1,0:T(8,128)S(1)} %get-tuple-element.7.gbc_ref, f32[20,128]{1,0:T(8,128)S(1)} %get-tuple-element.8.gstep_ref), custom_call_target="tpu_custom_call" | custom-call | tf_op jit(solution)/shard_map/pallas_call | solution.py:647

commit v4 on v3

--- a/solution.py
+++ b/solution.py
@@ -13,8 +13,10 @@
 BF16 = jnp.bfloat16
 HEAD_PAD = 32
 SKEW = 4
-LAG = 2
-EARLY = 2
+FOLLOW_FORWARD = 3
+FOLLOW_BACK = 4
+WORK_EVERY = 30
+DIRECT = 2
 SPAN = 125.0
 TOP_ROWS = 8
 
@@ -75,7 +77,7 @@
     code_fo, code_fi, code_bo, code_bi,
     near_x, near_b, near_step, next_dy, next_c, next_step, pads, weights, sides,
     xs_h, xs_l, ys_h, ys_l, xc, dyc, ec, ed, gain_row,
-    stp, rates, gains, cums, bc_acc, dcum_acc, dir_acc, sm, bcm,
+    stp, rates, gains, cums, bc_acc, dcum_acc, dir_acc, sm, bcm, turned,
     rate_sm, gain_sm, own_sem, send_sem, recv_x, recv_b, recv_f, recv_g, recv_r, recv_n,
 ):
     me = lax.axis_index("tp")
@@ -92,21 +94,34 @@
     has_prev = block > 0
     has_next = block < blocks - 1
 
+    mirror = peers - 1 - me
+    if peers % 2 == 0:
+        partners = [mirror]
+        for i in range(2, peers, 2):
+            partners += [lax.rem(me + i, peers), lax.rem(mirror + i, peers)]
+    else:
+        partners = [lax.rem(me + d, peers) for d in range(1, peers)]
+
     barrier = pltpu.get_barrier_semaphore()
-    for d in range(1, peers):
-        pl.semaphore_signal(
-            barrier, inc=1, device_id={"tp": lax.rem(me + d, peers)}, device_id_type=MESH
-        )
-
-    @pl.when(has_prev)
-    def _():
-        pl.semaphore_signal(barrier, inc=1, device_id={"seq": block - 1}, device_id_type=MESH)
-
-    @pl.when(has_next)
-    def _():
-        pl.semaphore_signal(barrier, inc=1, device_id={"seq": block + 1}, device_id_type=MESH)
-
-    neighbours = jnp.where(has_prev, 1, 0) + jnp.where(has_next, 1, 0)
+    for peer in partners:
+        pl.semaphore_signal(barrier, inc=1, device_id={"tp": peer}, device_id_type=MESH)
+
+    def greet(there, exists, wide):
+        @pl.when(jnp.logical_and(exists, wide))
+        def _():
+            for peer in range(peers):
+                pl.semaphore_signal(
+                    barrier, inc=1, device_id={"seq": there, "tp": peer}, device_id_type=MESH
+                )
+
+        @pl.when(jnp.logical_and(exists, jnp.logical_not(wide)))
+        def _():
+            pl.semaphore_signal(barrier, inc=1, device_id={"seq": there}, device_id_type=MESH)
+
+        return jnp.where(exists, jnp.where(wide, peers, 1), 0)
+
+    greeted = greet(block - 1, has_prev, jnp.logical_or(block == 1, block == blocks - 1))
+    greeted += greet(block + 1, has_next, jnp.logical_or(block == 0, block == blocks - 2))
 
     own_bc = pltpu.make_async_copy(bc_ref, bcr.at[me], own_sem.at[0])
     load_x = pltpu.make_async_copy(x_ref, x_in, own_sem.at[1])
@@ -142,11 +157,8 @@
         )
 
     own_bc.wait()
-    pl.semaphore_wait(barrier, peers - 1 + neighbours)
-    for d in range(1, peers):
-        bc_copy(lax.rem(me + d, peers), me).start()
-
-    early = min(EARLY, groups)
+    load_step.wait()
+    pl.semaphore_wait(barrier, peers - 1 + greeted)
 
     def lend(source, target, slot, sem, there):
         return pltpu.make_async_remote_copy(
@@ -154,35 +166,75 @@
             device_id={"seq": there}, device_id_type=MESH,
         )
 
-    def group_of(g):
-        return pl.ds(pl.multiple_of(g * group_lanes, 128), group_lanes)
-
-    def lend_x(g):
-        part = (slice(None), slice(None), group_of(g))
-        return lend(xr.at[part], near_x.at[part], 7, recv_f.at[g * group_chunks], block + 1)
-
-    def lend_dy(g):
-        part = (slice(None), group_of(g))
-        return lend(dy_in.at[part], next_dy.at[part], 8, recv_g.at[g * group_chunks], block - 1)
-
-    load_step.wait()
+    def lend_row(q, target, slot, sem, peer, there):
+        return pltpu.make_async_remote_copy(
+            src_ref=bcr.at[me, q], dst_ref=target.at[me],
+            send_sem=send_sem.at[slot], recv_sem=sem,
+            device_id={"seq": there, "tp": peer}, device_id_type=MESH,
+        )
 
     @pl.when(block == 0)
     def _():
         lend(step_in, near_step, 9, recv_n.at[2], block + 1).start()
-
-    load_dy.wait()
+        for peer in (*partners, me):
+            lend_row(0, near_b, 6, recv_n.at[0], peer, block + 1).start()
 
     @pl.when(block == blocks - 1)
     def _():
         lend(step_in, next_step, 10, recv_n.at[3], block - 1).start()
-        for g in range(early):
-            lend_dy(g).start()
+        for peer in (*partners, me):
+            lend_row(1, next_c, 11, recv_n.at[1], peer, block - 1).start()
+
+    for peer in partners:
+        bc_copy(peer, me).start()
+
+    direct = min(DIRECT, groups)
+
+    def lend_x(c, slot):
+        part = (slot, slice(None), pl.ds(c * lanes, lanes))
+        return lend(xr.at[part], near_x.at[part], 7, recv_f.at[c], block + 1)
+
+    def lend_own_x():
+        part = (me, slice(None), pl.ds(direct * group_lanes, width - direct * group_lanes))
+        return lend(xr.at[part], near_x.at[part], 7, recv_n.at[4], block + 1)
+
+    def lend_direct(c, peer):
+        start = pl.multiple_of(peer * width + c * lanes, 128)
+        return pltpu.make_async_remote_copy(
+            src_ref=x_in.at[:, pl.ds(start, lanes)],
+            dst_ref=near_x.at[me, :, pl.ds(c * lanes, lanes)],
+            send_sem=send_sem.at[7], recv_sem=recv_f.at[c],
+            device_id={"seq": block + 1, "tp": peer}, device_id_type=MESH,
+        )
+
+    def lend_dy(c):
+        part = (slice(None), pl.ds(c * lanes, lanes))
+        return lend(dy_in.at[part], next_dy.at[part], 8, recv_g.at[c], block - 1)
+
+    load_dy.wait()
+
+    @pl.when(block == blocks - 1)
+    def _():
+        for c in range(chunks):
+            lend_dy(c).start()
 
     load_x.wait()
+    own_x.wait()
     for g in range(groups):
-        for d in range(1, peers):
-            x_copy(lax.rem(me + d, peers), me, g).start()
+        if g < direct:
+            @pl.when(block == 0)
+            def _():
+                for c in range(g * group_chunks, (g + 1) * group_chunks):
+                    for peer in (*partners, me):
+                        lend_direct(c, peer).start()
+
+        if g == direct:
+            @pl.when(block == 0)
+            def _():
+                lend_own_x().start()
+
+        for peer in partners:
+            x_copy(peer, me, g).start()
 
     load_rate.wait()
     load_gain.wait()
@@ -261,57 +313,35 @@
         for c in range(chunks):
             weights[k, c] = dot2l(table, spread(c, 0))
 
-    @pl.when(block == 1)
-    def _():
-        borrow(
-            0, near_step,
-            lambda cum, steps: jnp.exp(cum[:, tokens - 1 : tokens] - cum) * steps,
-        )
-
-    @pl.when(block == blocks - 2)
-    def _():
-        borrow(1, next_step, lambda cum, steps: jnp.exp(cum))
-
-    landing(bcr.at[pl.ds(0, peers - 1)], recv_b.at[0], 0).wait_recv()
-
-    @pl.when(block == 0)
-    def _():
-        lend(bcr.at[:, 0], near_b, 6, recv_n.at[0], block + 1).start()
-
-    @pl.when(block == blocks - 1)
-    def _():
-        lend(bcr.at[:, 1], next_c, 11, recv_n.at[1], block - 1).start()
-        for g in range(early, groups):
-            lend_dy(g).start()
-
-    proj_b = bcr[:, 0].reshape(tokens, -1)
-    proj_c = bcr[:, 1].reshape(tokens, -1)
-    bcm[0] = proj_b
-    bcm[1] = proj_c
-    c_t = proj_c.astype(F32).T.astype(BF16)
-    for c in range(chunks):
-        pulled[c] = dot2(c_t, (ys_h[c], ys_l[c]))
-
-    b_t = proj_b.astype(F32).T.astype(BF16)
-    scores_t = jnp.where(upto, dot(proj_b, proj_c, NT), 0.0)
-    sm[0], sm[1] = split(scores_t)
-    sm[2], sm[3] = split(scores_t.T)
-
-    @pl.when(jnp.logical_not(has_next))
-    def _():
-        pull_in[...] = jnp.zeros_like(pull_in)
-
-    dcum_acc[...] = jnp.zeros_like(dcum_acc)
-    dir_acc[...] = jnp.zeros_like(dir_acc)
-
-    own_x.wait()
-    for g in range(groups):
+    def borrow_side(k, side):
+        landing(side, recv_n.at[k], 0).wait_recv()
+        sides[k] = side[...].reshape(tokens, -1).astype(F32).T.astype(BF16)
+
+    def gather_bc():
+        landing(bcr.at[pl.ds(0, peers - 1)], recv_b.at[0], 0).wait_recv()
+        proj_b = bcr[:, 0].reshape(tokens, -1)
+        proj_c = bcr[:, 1].reshape(tokens, -1)
+        bcm[0] = proj_b
+        bcm[1] = proj_c
+        turned[0] = proj_b.astype(F32).T.astype(BF16)
+        turned[1] = proj_c.astype(F32).T.astype(BF16)
+        scores_t = jnp.where(upto, dot(proj_b, proj_c, NT), 0.0)
+        sm[0], sm[1] = split(scores_t)
+        sm[2], sm[3] = split(scores_t.T)
+
+    def pull_all():
+        for c in range(chunks):
+            pulled[c] = dot2(turned[1], (ys_h[c], ys_l[c]))
+
+    def take_x(g):
         group = xr.at[pl.ds(0, peers - 1), :, pl.ds(g * group_lanes, group_lanes)]
         landing(group, recv_x.at[g], 1).wait_recv()
-
-        @pl.when(block == 0)
-        def _():
-            lend_x(g).start()
+        if g >= direct:
+            @pl.when(block == 0)
+            def _():
+                for c in range(g * group_chunks, (g + 1) * group_chunks):
+                    for peer in partners:
+                        lend_x(c, peer).start()
 
         for c in range(g * group_chunks, (g + 1) * group_chunks):
             x = xr[:, :, c * lanes : (c + 1) * lanes].reshape(tokens, lanes)
@@ -319,7 +349,14 @@
             pair = split(ed[c] * x.astype(F32))
             xs_h[c] = pair[0]
             xs_l[c] = pair[1]
-            fresh[c] = dot2(b_t, pair)
+            fresh[c] = dot2(turned[0], pair)
+
+    @pl.when(jnp.logical_not(has_next))
+    def _():
+        pull_in[...] = jnp.zeros_like(pull_in)
+
+    dcum_acc[...] = jnp.zeros_like(dcum_acc)
+    dir_acc[...] = jnp.zeros_like(dir_acc)
 
     def finish_inner():
         inner = jnp.zeros((tokens, tokens), F32)
@@ -340,8 +377,8 @@
         )
 
     def send_sums(q):
-        for d in range(1, peers):
-            sum_copy(q, lax.rem(me + d, peers), me).start()
+        for peer in partners:
+            sum_copy(q, peer, me).start()
 
     def selector(c):
         head = lax.broadcasted_iota(jnp.int32, (HEAD_PAD, lanes), 0)
@@ -352,13 +389,18 @@
         return dot2(sides[k], split(weights[k, c] * values.astype(F32)))
 
     def part_of(c):
+        if isinstance(c, int):
+            return pl.ds(c * lanes, lanes)
         return pl.ds(pl.multiple_of(c * lanes, 128), lanes)
 
-    def forward_input(kind, c, opens):
+    def forward_input(kind, c):
         if kind == "raw":
-            if opens:
-                group = near_x.at[:, :, pl.ds(0, group_lanes)]
-                landing(group, recv_f.at[c], 0).wait_recv()
+            if c == direct * group_chunks:
+                rest = width - c * lanes
+                landing(near_x.at[0, :, pl.ds(0, rest)], recv_n.at[4], 0).wait_recv()
+            count = peers if c < direct * group_chunks else peers - 1
+            part = near_x.at[pl.ds(0, count), :, pl.ds(0, lanes)]
+            landing(part, recv_f.at[c], 0).wait_recv()
             entering = rebuilt(0, c, near_x[:, :, part_of(c)].reshape(tokens, lanes))
         else:
             forward_copy(c).wait_recv()
@@ -366,10 +408,9 @@
         state_in[c] = entering
         return entering
 
-    def backward_input(kind, c, opens):
+    def backward_input(kind, c):
         if kind == "raw":
-            if opens:
-                landing(next_dy.at[:, pl.ds(0, group_lanes)], recv_g.at[c], 0).wait_recv()
+            landing(next_dy.at[:, pl.ds(0, lanes)], recv_g.at[c], 0).wait_recv()
             arriving = rebuilt(1, c, next_dy[:, part_of(c)])
         else:
             backward_copy(c).wait_recv()
@@ -377,19 +418,20 @@
         pull_in[c] = arriving
         return arriving
 
-    def forward_link(kind, sends, c, opens):
+    def forward_link(kind, sends, c):
         if kind == "none":
             state_out[c] = total_decay(c) * fresh[c]
             return
-        leaving = total_decay(c) * (forward_input(kind, c, opens) + fresh[c])
+
+        leaving = total_decay(c) * (forward_input(kind, c) + fresh[c])
         state_out[c] = leaving
         if sends:
             send_forward(c, leaving)
 
-    def backward_link(kind, sends, c, opens):
+    def backward_link(kind, sends, c):
         if kind == "none":
             return
-        arriving = backward_input(kind, c, opens)
+        arriving = backward_input(kind, c)
         if sends:
             send_backward(c, total_decay(c) * arriving + pulled[c])
 
@@ -407,8 +449,7 @@
         if kind != "none":
             left, right = (*left, bcm[1], bcm[1]), (*right, *split(state_in[c]))
         z = joined(left, right)
-        v = split(ec[c] * dyc[c].astype(F32) * z)
-        dcum_acc[...] += dot2(selector(c), v, NT)
+        dcum_acc[...] += dot2(selector(c), split(dyc[c].astype(F32) * z), NT)
 
     def backward_work(kind, c):
         left, right = (sm[0], sm[0], sm[1]), (ys_h[c], ys_l[c], ys_h[c])
@@ -417,13 +458,9 @@
             left, right = (*left, bcm[0], bcm[0]), (*right, *leaving)
         a2 = joined(left, right)
         x = xc[c].astype(F32)
-        growth = ed[c]
-        gx = growth * a2 + gain_row[c, 0:1, :] * dyc[c].astype(F32)
+        gx = ed[c] * a2 + gain_row[c, 0:1, :] * dyc[c].astype(F32)
         gx_ref[:, part_of(c)] = gx.astype(BF16)
-        direct = x * a2
-        pick = selector(c)
-        dir_acc[...] += dot2(pick, split(direct), NT)
-        dcum_acc[...] -= dot2(pick, split(growth * direct), NT)
+        dir_acc[...] += dot2(selector(c), split(x * a2), NT)
 
     def grouped(part, *fixed):
         def run(g):
@@ -431,12 +468,6 @@
                 part(*fixed, g * group_chunks + i)
         return run
 
-    def grouped_link(part, kind, sends):
-        def run(g):
-            for i in range(group_chunks):
-                part(kind, sends, g * group_chunks + i, i == 0)
-        return run
-
     def loop(low, high, *parts):
         def body(k, carry):
             for part, shift in parts:
@@ -446,35 +477,54 @@
         if high > low:
             lax.fori_loop(low, high, body, 0)
 
-    def edge_role(links, sums, work, other_work, early, late):
+    def edge_role(link, add, work, other_work, early, late, flat):
+        def take(g):
+            for i in range(group_chunks):
+                link(g * group_chunks + i)
+                add(g * group_chunks + i)
+
         finish_inner()
         send_sums(early)
         loop(0, groups, (other_work, 0))
-        loop(0, groups - 1, (links, 0), (sums, 0), (work, 0))
-        links(groups - 1)
-        sums(groups - 1)
+        if flat:
+            for g in range(groups - 1):
+                take(g)
+                work(g)
+        else:
+            loop(0, groups - 1, (take, 0), (work, 0))
+        take(groups - 1)
         send_sums(late)
         work(groups - 1)
 
-    def inner_role(lead, follow, lag):
-        (link1, sum1, work1), (link2, sum2, work2) = lead, follow
-        ahead = min(lag, groups)
-        rest = groups - ahead
-        both = min(ahead, rest)
-        loop(0, ahead, (link1, 0), (sum1, 0), (work1, 0))
-        loop(ahead, groups, (link1, 0), (link2, -ahead))
-        loop(
-            rest, rest + both, (link2, 0), (sum1, ahead - rest), (work1, ahead - rest),
-            (sum2, -rest), (work2, -rest),
-        )
-        loop(rest + both, groups, (link2, 0), (sum2, -rest), (work2, -rest))
-        loop(ahead + both, groups, (sum1, 0))
-        loop(ahead, groups, (sum2, 0))
+    def inner_role(lead, follow, behind, done):
+        (link1, add1, work1), (link2, add2, work2) = lead, follow
+        links, adds, works = (link1, link2), (add1, add2), (work1, work2)
+        steps = [(0, c) for c in range(chunks)]
+        for c in reversed(range(chunks)):
+            steps.insert(min(chunks, behind + 3 * c // 2 + 1), (1, c))
+        ready = [(0, c) for c in range(group_chunks - 1, done, group_chunks)]
+        steps = [step for step in steps if step not in [(0, c) for c in range(done)]]
+
+        def add_group(side, g):
+            for c in range(g * group_chunks, (g + 1) * group_chunks):
+                adds[side](c)
+
+        for at, (side, c) in enumerate(steps):
+            links[side](c)
+            if c % group_chunks == group_chunks - 1:
+                ready.append((side, c))
+            leading = any(other == 0 for other, _ in steps[at + 1 :])
+            if ready and (not leading or at % WORK_EVERY == WORK_EVERY - 1):
+                other, last = ready.pop(0)
+                add_group(other, last // group_chunks)
+                works[other](last // group_chunks)
+        for side, last in ready:
+            add_group(side, last // group_chunks)
         finish_inner()
         send_sums(0)
         send_sums(1)
-        loop(ahead + both, groups, (work1, 0))
-        loop(ahead, groups, (work2, 0))
+        for side, last in ready:
+            works[side](last // group_chunks)
 
     def between(s, carry):
         cf = s - SKEW * (block - 1)
@@ -482,13 +532,13 @@
 
         @pl.when(jnp.logical_and(cf >= 0, cf < chunks))
         def _():
-            forward_link("code", True, cf, True)
+            forward_link("code", True, cf)
             forward_sum("code", cf)
             forward_work("code", cf)
 
         @pl.when(jnp.logical_and(cb >= 0, cb < chunks))
         def _():
-            backward_link("code", True, cb, True)
+            backward_link("code", True, cb)
             backward_sum("code", cb)
             backward_work("code", cb)
 
@@ -500,35 +550,58 @@
         def _():
             forward = "none" if b == 0 else "raw" if b == 1 else "code"
             backward = "none" if b == blocks - 1 else "raw" if b == blocks - 2 else "code"
-            if forward == "raw":
-                landing(near_b, recv_n.at[0], 0).wait_recv()
-                sides[0] = near_b[...].reshape(tokens, -1).astype(F32).T.astype(BF16)
-            if backward == "raw":
-                landing(next_c, recv_n.at[1], 0).wait_recv()
-                sides[1] = next_c[...].reshape(tokens, -1).astype(F32).T.astype(BF16)
             sends = forward != "none" and backward != "none"
             ahead = (
-                grouped_link(forward_link, forward, sends),
-                grouped(forward_sum, forward), grouped(forward_work, forward),
+                partial(forward_link, forward, sends),
+                partial(forward_sum, forward), grouped(forward_work, forward),
             )
             behind = (
-                grouped_link(backward_link, backward, sends),
-                grouped(backward_sum, backward), grouped(backward_work, backward),
+                partial(backward_link, backward, sends),
+                partial(backward_sum, backward), grouped(backward_work, backward),
             )
+            lag = (blocks - 2 - b) - (b - 1)
+            if forward == "raw":
+                borrow(
+                    0, near_step,
+                    lambda cum, steps: jnp.exp(cum[:, tokens - 1 : tokens] - cum) * steps,
+                )
+            if backward == "raw":
+                borrow(1, next_step, lambda cum, steps: jnp.exp(cum))
+            gather_bc()
+            if sends:
+                pull_all()
+            if forward == "raw":
+                borrow_side(0, near_b)
+            if backward == "raw":
+                borrow_side(1, next_c)
+            done = 0
+            if sends and lag < 0:
+                done = group_chunks
+                for c in range(done):
+                    behind[0](c)
+            for g in range(groups):
+                take_x(g)
+                if sends and lag > 0 and g < direct:
+                    done = (g + 1) * group_chunks
+                    for c in range(g * group_chunks, done):
+                        ahead[0](c)
             if forward == "none":
-                loop(0, groups, (ahead[0], 0))
-                edge_role(*behind, ahead[2], 1, 0)
+                loop(0, groups, (grouped(ahead[0]), 0))
+                edge_role(*behind, ahead[2], 1, 0, backward == "raw")
             elif backward == "none":
-                edge_role(*ahead, behind[2], 0, 1)
+                edge_role(*ahead, behind[2], 0, 1, forward == "raw")
+            elif lag < 0:
+                inner_role(behind, ahead, FOLLOW_FORWARD - 3 * (lag + 1), done)
             else:
-                lag = LAG * ((blocks - 2 - b) - (b - 1))
-                if lag < 0:
-                    ahead, behind = behind, ahead
-                inner_role(ahead, behind, abs(lag))
+                inner_role(ahead, behind, FOLLOW_BACK + 3 * max(lag - 1, 0), done)
 
     if blocks > 4:
         @pl.when(jnp.logical_and(block > 1, block < blocks - 2))
         def _():
+            gather_bc()
+            pull_all()
+            for g in range(groups):
+                take_x(g)
             lax.fori_loop(0, chunks + SKEW * (blocks - 3), between, 0)
             finish_inner()
             send_sums(1)
@@ -539,15 +612,17 @@
         both = (pull_in[c] * state_out[c]).reshape(-1, 8, lanes).sum(axis=0)
         edge = edge + dot2(selector(c), split(both), NT)
     edge = jnp.sum(edge, axis=1, keepdims=True)
-    after = exact(dcum_acc[...], jnp.where(row >= col, 1.0, 0.0).astype(F32)) + edge
-    gstep = jnp.exp(-cums[...]) * dir_acc[...] - rates[...] * after
+    growth = jnp.exp(-cums[...])
+    dcum = jnp.exp(cums[...]) * dcum_acc[...] - growth * stp[...] * dir_acc[...]
+    after = exact(dcum, jnp.where(row >= col, 1.0, 0.0).astype(F32)) + edge
+    gstep = growth * dir_acc[...] - rates[...] * after
     gstep_ref[...] = gstep[0:head_count]
 
     for q in range(2):
         landing(rs.at[q, pl.ds(0, peers - 1)], recv_r.at[q], 4 + q).wait_recv()
         total = bc_acc[q, pl.ds(pl.multiple_of(me * rows, 8), rows)]
-        for d in range(1, peers):
-            total = total + rs[q, lax.rem(me + d, peers)]
+        for peer in partners:
+            total = total + rs[q, peer]
         gbc_ref[q] = total
 
     landing(bcr.at[pl.ds(0, peers - 1)], recv_b.at[0], 0).wait_send()
@@ -639,8 +714,9 @@
             heads, heads,
             pltpu.VMEM((4, tokens, tokens), BF16),
             pltpu.VMEM((2, tokens, state), BF16),
+            pltpu.VMEM((2, state, tokens), BF16),
             pltpu.SMEM((head_count,), F32), pltpu.SMEM((head_count,), F32),
-            dma(7), dma(12), dma(groups), dma(1), dma(chunks), dma(chunks), dma(2), dma(4),
+            dma(7), dma(12), dma(groups), dma(1), dma(chunks), dma(chunks), dma(2), dma(5),
         ],
         compiler_params=pltpu.CompilerParams(collective_id=0, has_side_effects=True),
     )(x_ckpt, bc_ckpt, step_sizes, decay_rate, skip_gain, grad_out)

time: 30 us -> 28.8 us (0.960)
  Pallas kernels: 29.1 us -> 27.8 us
    pallas_call x1, Pallas kernels: 28.3 us -> 27 us  [shards(): pl.pallas_call(partial(kernel, peers, blocks, head_width), out_shape=tupl...]
where the time goes in v4:
time: 28.8 us; the launch traced here: 28.6 us
  Pallas kernels  27.8 us (97%)
  between operations  0.8 us (3%)
    pallas_call x1, Pallas kernels, shards(): pl.pallas_call(partial(kernel, peers, blocks, head_width), out_shape=tupl...  27 us
    pallas_call x1, Pallas kernels, shards(): pl.pallas_call(store, out_shape=tuple((jax.ShapeDtypeStruct(shape, dtype)...  0.76 us

profile of v4, /device:TPU:0, one launch (start us, length us, event | category | flops | bytes accessed | tf_op | source)
XLA Modules:
  0.0 28.6 jit_solution(903823097241976359)
XLA Ops:
  0.6 27.0 %shard_map.85 = (bf16[128,1280]{1,0:T(8,128)(2,1)S(1)}, f32[2,32,128]{2,1,0:T(8,128)S(1)}, f32[20,128]{1,0:T(8,128)S(1)}) custom-call(bf16[32,5120]{1,0:T(8,128)(2,1)} %x_ref.1, bf16[2,32,128]{2,1,0:T(8,128)(2,1)} %bc_ref.1, f32[20,128]{1,0:T(8,128)} %step_ref.1, f32[20]{0:T(128)} %rate_ref.1, f32[20]{0:T(128)} %gain_ref.1, bf16[128,1280]{1,0:T(8,128)(2,1)} %dy_ref.1), custom_call_target="tpu_custom_call" | custom-call | tf_op jit(solution)/shard_map/pallas_call | solution.py:686
  27.7 0.8 %shard_map.86 = (bf16[128,1280]{1,0:T(8,128)(2,1)}, f32[2,32,128]{2,1,0:T(8,128)}, f32[20,128]{1,0:T(8,128)}) custom-call(bf16[128,1280]{1,0:T(8,128)(2,1)S(1)} %get-tuple-element.6.gx_ref, f32[2,32,128]{2,1,0:T(8,128)S(1)} %get-tuple-element.7.gbc_ref, f32[20,128]{1,0:T(8,128)S(1)} %get-tuple-element.8.gstep_ref), custom_call_target="tpu_custom_call" | custom-call | tf_op jit(solution)/shard_map/pallas_call | solution.py:723

commit v5 on v4

--- a/solution.py
+++ b/solution.py
@@ -13,8 +13,9 @@
 BF16 = jnp.bfloat16
 HEAD_PAD = 32
 SKEW = 4
-FOLLOW_FORWARD = 3
+FOLLOW_FORWARD = 5
 FOLLOW_BACK = 4
+FIRST_BACK = 3
 WORK_EVERY = 30
 DIRECT = 2
 SPAN = 125.0
@@ -576,7 +577,7 @@
                 borrow_side(1, next_c)
             done = 0
             if sends and lag < 0:
-                done = group_chunks
+                done = min(FIRST_BACK, groups) * group_chunks
                 for c in range(done):
                     behind[0](c)
             for g in range(groups):

time: 28.8 us -> 27.6 us (0.958)
  Pallas kernels: 27.8 us -> 26.5 us
    pallas_call x1, Pallas kernels: 27 us -> 25.8 us  [shards(): pl.pallas_call(partial(kernel, peers, blocks, head_width), out_shape=tupl...]
where the time goes in v5:
time: 27.6 us; the launch traced here: 27.3 us
  Pallas kernels  26.5 us (96%)
  between operations  0.8 us (3%)
    pallas_call x1, Pallas kernels, shards(): pl.pallas_call(partial(kernel, peers, blocks, head_width), out_shape=tupl...  25.8 us
    pallas_call x1, Pallas kernels, shards(): pl.pallas_call(store, out_shape=tuple((jax.ShapeDtypeStruct(shape, dtype)...  0.76 us

profile of v5, /device:TPU:0, one launch (start us, length us, event | category | flops | bytes accessed | tf_op | source)
XLA Modules:
  0.0 27.3 jit_solution(12323929460988835038)
XLA Ops:
  0.6 25.8 %shard_map.85 = (bf16[128,1280]{1,0:T(8,128)(2,1)S(1)}, f32[2,32,128]{2,1,0:T(8,128)S(1)}, f32[20,128]{1,0:T(8,128)S(1)}) custom-call(bf16[32,5120]{1,0:T(8,128)(2,1)} %x_ref.1, bf16[2,32,128]{2,1,0:T(8,128)(2,1)} %bc_ref.1, f32[20,128]{1,0:T(8,128)} %step_ref.1, f32[20]{0:T(128)} %rate_ref.1, f32[20]{0:T(128)} %gain_ref.1, bf16[128,1280]{1,0:T(8,128)(2,1)} %dy_ref.1), custom_call_target="tpu_custom_call" | custom-call | tf_op jit(solution)/shard_map/pallas_call | solution.py:687
  26.4 0.8 %shard_map.86 = (bf16[128,1280]{1,0:T(8,128)(2,1)}, f32[2,32,128]{2,1,0:T(8,128)}, f32[20,128]{1,0:T(8,128)}) custom-call(bf16[128,1280]{1,0:T(8,128)(2,1)S(1)} %get-tuple-element.6.gx_ref, f32[2,32,128]{2,1,0:T(8,128)S(1)} %get-tuple-element.7.gbc_ref, f32[20,128]{1,0:T(8,128)S(1)} %get-tuple-element.8.gstep_ref), custom_call_target="tpu_custom_call" | custom-call | tf_op jit(solution)/shard_map/pallas_call | solution.py:724
